TPU v7x, 256 devices: a whole 4x4x8 slice. The times are simulated.
256 devices in a mesh: dp: 32 (over x, y, core), tensor: 8 (over z).
Axes of the slice: x: 4, y: 4, z: 8, core: 2. Of those that a mesh axis runs over, the one named last changes fastest.
Arguments:
- query: bfloat16 [512, 4096], P('dp', 'tensor'), may hold values from -8000 to 8000
- incoming_key: bfloat16 [512, 2048], P('dp', 'tensor'), may hold values from -4.5 to 4.5
- new_value: bfloat16 [512, 2048], P('dp', 'tensor'), may hold values from -4.5 to 4.5
- key_cache: bfloat16 [512, 256, 2048], P('dp', None, 'tensor'), may hold values from -4.5 to 4.5
- value_cache: bfloat16 [512, 256, 2048], P('dp', None, 'tensor'), may hold values from -4.5 to 4.5
- cache_len: int32 [512], P('dp'), may hold values from 2 to 256
- out_weight: bfloat16 [4096, 4608], P('tensor'), may hold values from -0.09375 to 0.09375
- residual: bfloat16 [512, 4608], P('dp'), may hold values from -6 to 6
- post_gain: float32 [4608], replicated, may hold values from 0.5 to 1.5
- final_gain: float32 [4608], replicated, may hold values from 0.5 to 1.5
- vocab_weight: bfloat16 [131072, 4608], P(('dp', 'tensor')), may hold values from -113 to 113
- sampled: int32 [512], P('dp'), may hold values from 0 to 131071
- stop_flag: int32 [512], P('dp'), may hold values from 0 to 1, as said below
Outputs:
- new_residual: bfloat16 [512, 4608], P('dp', 'tensor')
- token_logprob: float32 [512], P('dp')
- insert_rank: int32 [512], P('dp')
- released_slot_total: int32 [], replicated
Inputs may be any that keep to these rules, and one draw needn't show every extreme that they name: `stop_flag`: each aligned block of 16 slots holds 1 to 16 stops.
All inputs are finite; a program needn't handle non-finite values.
Results may differ from a plain program's by a relative error of at most 0.0038.
The roundings to bfloat16 on the way count: a program that leaves them out, or rounds other values in their place, can miss the bound.
Values may be sent and summed in bfloat16 or wider, within the bound.
No kernel may reach another device: no remote copies, remote signals or barrier semaphores. Data moves between devices by JAX's collectives and lax.ppermute only.
A program may use at most 64 MiB of HBM per device.

v0:
```python
import jax
import jax.numpy as jnp
from jax import lax
from jax.sharding import Mesh
from jax.sharding import PartitionSpec as P

D = 4608
HEADS = 32
KV_HEADS = 16
HEAD_DIM = 128
DP = ("dp_0", "dp_1", "dp_2")
DP_TENSOR = ("dp_0", "dp_1", "dp_2", "tensor")


def gathered_total(shard, axis):
    return lax.all_gather(shard, axis).sum(0)


def all_in_one(shard, axis):
    leaves = jax.tree.leaves(shard)
    sequence = sorted(range(len(leaves)), key=lambda k: -leaves[k].size)
    width = (1, *leaves[sequence[0]].shape)[-1]
    lines = [
        jnp.pad(leaves[k].reshape(-1), (0, -leaves[k].size % width)).reshape(-1, width)
        for k in sequence
    ]
    both, at, found = (lax.all_gather(jnp.concatenate(lines), axis), 0, {})
    for k, line in zip(sequence, lines):
        share = both[:, at : at + len(line)].reshape(len(both), -1)
        found[k] = share[:, : leaves[k].size].reshape(-1, *leaves[k].shape)
        at += len(line)
    numbers = iter(range(len(leaves)))
    return jax.tree.map(lambda _: found[next(numbers)], shard)


def combined_by_axis(shard, axes, combine):
    for axis in axes:
        pieces = all_in_one(shard, axis)
        shard = jax.tree.map(lambda part: part[0], pieces)
        for k in range(1, lax.axis_size(axis)):
            shard = combine(shard, jax.tree.map(lambda part: part[k], pieces))
    return shard


def attend_local(query, incoming_key, new_value, key_cache, value_cache, cache_len):
    slot_dev = query.shape[0]
    positions = key_cache.shape[1]
    kv_local = incoming_key.shape[1] // HEAD_DIM
    group = HEADS // KV_HEADS
    query_vector = query.reshape(slot_dev, kv_local, group, HEAD_DIM)
    keys = key_cache.reshape(slot_dev, positions, kv_local, HEAD_DIM)
    values = value_cache.reshape(slot_dev, positions, kv_local, HEAD_DIM)
    self_key = incoming_key.reshape(slot_dev, kv_local, HEAD_DIM)
    own_value = new_value.reshape(slot_dev, kv_local, HEAD_DIM).astype(jnp.float32)
    scores = (
        jnp.einsum("bkgd,bckd->bkgc", query_vector, keys, preferred_element_type=jnp.float32) / 12.0
    )
    self_entry = (
        jnp.einsum("qyxm,qym->qyx", query_vector, self_key, preferred_element_type=jnp.float32)
        / 12.0
    )
    valid = (
        jnp.arange(positions, dtype=jnp.int32)[None, None, None, :] < cache_len[:, None, None, None]
    )
    scores = jnp.where(valid, scores, -1e30)
    top = jnp.maximum(jnp.max(scores, axis=-1), self_entry)
    expo = jnp.where(valid, jnp.exp(scores - top[..., None]), 0.0)
    own_exp = jnp.exp(self_entry - top)
    total = jnp.sum(expo, axis=-1) + own_exp
    weight = (expo / total[..., None]).astype(jnp.bfloat16)
    own_weight = (own_exp / total).astype(jnp.bfloat16).astype(jnp.float32)
    attn = jnp.einsum("bkgc,bckd->bkgd", weight, values, preferred_element_type=jnp.float32)
    attn = attn + own_weight[..., None] * own_value[:, :, None, :]
    return attn.astype(jnp.bfloat16).reshape(slot_dev, kv_local * group * HEAD_DIM)


def collect_slots(hidden, sampled):
    return (
        lax.all_gather(hidden, DP, axis=0, tiled=True),
        lax.all_gather(sampled, DP, axis=0, tiled=True),
    )


def combine_stats(first, second):
    top = jnp.maximum(first[0], second[0])
    total = first[1] * jnp.exp(first[0] - top) + second[1] * jnp.exp(second[0] - top)
    return (top, total, first[2] + second[2], first[3] + second[3])


def on_device(
    query,
    incoming_key,
    new_value,
    key_cache,
    value_cache,
    cache_len,
    out_weight,
    residual,
    post_gain,
    final_gain,
    vocab_weight,
    sampled,
    stop_flag,
):
    slot_dev = query.shape[0]
    attn = attend_local(query, incoming_key, new_value, key_cache, value_cache, cache_len)
    partial_value = jnp.dot(attn, out_weight, preferred_element_type=jnp.float32)
    whole = gathered_total(partial_value, "tensor")
    post = whole * lax.rsqrt(jnp.mean(whole * whole, axis=1, keepdims=True) + 1e-06) * post_gain
    full_mix = (residual.astype(jnp.float32) + post).astype(jnp.bfloat16)
    mixed = full_mix.astype(jnp.float32)
    hidden = (
        mixed * lax.rsqrt(jnp.mean(mixed * mixed, axis=1, keepdims=True) + 1e-06) * final_gain
    ).astype(jnp.bfloat16)
    width = D // lax.axis_size("tensor")
    new_residual = lax.dynamic_slice_in_dim(full_mix, lax.axis_index("tensor") * width, width, 1)
    every, ids = collect_slots(hidden, sampled)
    logits = lax.dot_general(
        every, vocab_weight, (((1,), (1,)), ((), ())), preferred_element_type=jnp.float32
    )
    vocabulary_per_device = vocab_weight.shape[0]
    vocab_start = (
        lax.axis_index(DP) * lax.axis_size("tensor") + lax.axis_index("tensor")
    ) * vocabulary_per_device
    local_ids = ids - vocab_start
    hit = jnp.arange(vocabulary_per_device, dtype=jnp.int32)[None, :] == local_ids[:, None]
    picked_part = jnp.sum(jnp.where(hit, logits, 0.0), axis=1)
    row_max = jnp.max(logits, axis=1)
    freed = (stop_flag == 1).astype(jnp.int32)
    count = jnp.sum(freed)
    groups = lax.axis_size(DP)
    lane_ids = jnp.arange(groups, dtype=jnp.int32)
    first_core = (lax.axis_index("tensor") == 0).astype(jnp.float32)
    lanes = jnp.where(lane_ids == lax.axis_index(DP), count.astype(jnp.float32) * first_core, 0.0)
    local_sum = jnp.sum(jnp.exp(logits - row_max[:, None]), axis=1)
    top, expsum, picked, tallied_entries = combined_by_axis(
        (row_max, local_sum, picked_part, lanes), DP_TENSOR, combine_stats
    )
    before = jnp.sum(jnp.where(lane_ids < lax.axis_index(DP), tallied_entries, 0.0)).astype(
        jnp.int32
    )
    released_count = jnp.sum(tallied_entries).astype(jnp.int32)
    logprob_all = picked - (jnp.log(expsum) + top)
    token_logprob = lax.dynamic_slice_in_dim(
        logprob_all, lax.axis_index(DP) * slot_dev, slot_dev, 0
    )
    local_before = jnp.cumsum(freed) - freed + before
    insert_rank = jnp.where(freed == 1, local_before, -1)
    return (new_residual, token_logprob, insert_rank, released_count)


def solution(mesh):
    split = Mesh(
        mesh.devices.reshape(4, 4, 2, mesh.shape["tensor"]), ("dp_0", "dp_1", "dp_2", "tensor")
    )
    in_specs = (
        P(DP, "tensor"),
        P(DP, "tensor"),
        P(DP, "tensor"),
        P(DP, None, "tensor"),
        P(DP, None, "tensor"),
        P(DP),
        P("tensor", None),
        P(DP, None),
        P(),
        P(),
        P(DP_TENSOR, None),
        P(DP),
        P(DP),
    )
    out_specs = (P(DP, "tensor"), P(DP), P(DP), P())
    return jax.shard_map(
        on_device, mesh=split, in_specs=in_specs, out_specs=out_specs, check_vma=False
    )
```

profile of v0, /device:TPU:8, one launch (start us, length us, event | category | flops | bytes accessed | tf_op | source)
XLA Modules:
  0.0 184.2 jit_solution(2291557467032989353)
XLA Ops:
  7.2 0.0 copy-start
  7.2 0.0 copy-start.4
  7.2 0.0 all-gather.14.cloned.1.call-start
  7.2 0.9 reshape.784
  8.1 0.7 reshape.834
  8.8 0.7 iota_compare_fusion.1
  9.5 0.1 fusion.85
  9.7 0.0 copy-done
  9.7 0.7 fusion.83
  10.5 0.2 fusion.22
  10.7 0.0 copy-done.4
  10.8 2.0 %fusion.15 = bf16[16,2,2,128]{3,2,1,0:T(2,128)(2,1)S(1)} fusion(f32[16,2,2]{2,1,0:T(2,128)S(1)} %get-tuple-element.34, f32[16,2,128]{2,1,0:T(2,128)S(1)} %reshape.802, f32[16,2,2]{2,1,0:T(2,128)S(1)} %get-tuple-element.33, f32[16,2,2,256]{3,2,1,0:T(2,128)S(1)} %get-tuple-element.36, pred[16,256]{1,0:T(8,128)(4,1)S(1)} %iota_compare_fusion.1, ...), kind=kOutput, calls=%fused_computation.9 | convolution fusion | flops 4284416 | bytes 2200320 | tf_op jit(solution)/shard_map/bkgc,bckd->bkgd/dot_general | solution.py:72
  12.8 3.8 %fusion.86 = f32[16,4608]{1,0:T(8,128)} fusion(bf16[16,512]{1,0:T(8,128)(2,1)S(1)} %reshape.788, bf16[512,4608]{1,0:T(8,128)(2,1)} %param.19), kind=kOutput, calls=%fused_computation.160 | convolution fusion | flops 75497472 | bytes 5029888 | tf_op jit(solution)/shard_map/dot_general | solution.py:107
  16.6 0.0 copy-start.1
  16.6 0.0 copy-start.2
  16.6 0.0 copy-start.3
  16.6 0.0 all-gather.14.cloned.1.call-update
  16.6 0.0 copy-start.5
  16.7 0.0 copy-start.7
  16.7 0.0 copy-start.6
  16.7 0.0 all-gather.12.cloned.1.call-start
  16.7 44.1 %all-gather.14.cloned.1.call-done = f32[128,4608]{1,0:T(8,128)} async-done(((f32[16,4608]{1,0:T(8,128)}), f32[128,4608]{1,0:T(8,128)}) %all-gather.14.cloned.1.call-update) | async-done | bytes 2359312 | tf_op jit(solution)/shard_map/all_gather | solution.py:16
  60.9 1.8 reduce_sum.82
  62.7 0.2 multiply_reduce_fusion
  62.8 0.0 copy-done.1
  62.8 0.0 copy-done.2
  62.9 0.3 fusion.18
  63.1 0.0 copy-done.3
  63.1 0.8 fusion.20
  63.9 0.0 all-gather.12.cloned.1.call-update
  63.9 0.0 copy-done.5
  63.9 0.6 fusion.74
  65.3 0.1 copy.25
  65.4 0.1 reduce.1
  65.5 0.0 copy-done.7
  65.5 0.6 dynamic-slice
  66.8 0.0 copy-done.6
  66.8 0.2 dynamic-update-slice
  67.0 15.4 %all-reduce.4 = s32[512]{0:T(512)S(1)} all-reduce(s32[512]{0:T(512)S(1)} %dynamic-update-slice), channel_id=1, replica_groups=mesh['dp_0'=4,'dp_1'=4,'dp_2'=2,'tensor'=8] {'dp_0','dp_1','dp_2'}, use_global_device_ids=true, to_apply=%add.4 | all-reduce | flops 512 | bytes 4096
  82.5 0.7 constant_dynamic-slice_fusion
  83.2 31.0 %all-gather.12.cloned.1.call-done = bf16[512,4608]{1,0:T(8,128)(2,1)} async-done(((bf16[16,4608]{1,0:T(8,128)(2,1)}), bf16[512,4608]{1,0:T(8,128)(2,1)}) %all-gather.12.cloned.1.call-update) | async-done | bytes 4718608 | tf_op jit(solution)/shard_map/all_gather | solution.py:79
  114.2 5.9 %fusion.84 = (f32[512]{0:T(512)S(1)}, f32[512,512]{0,1:T(8,128)S(1)}) fusion(bf16[512,4608]{1,0:T(8,128)(2,1)} %all-gather.12.cloned.1.call-done, bf16[512,4608]{1,0:T(8,128)(2,1)} %param.23), kind=kOutput, calls=%fused_computation.158 | convolution fusion | flops 2416180736 | bytes 10487808 | tf_op jit(solution)/shard_map/dot_general | solution.py:118
  120.1 0.3 exponential_reduce_fusion
  120.4 11.9 %all-gather.5 = f32[4,4,512]{2,1,0:T(4,128)S(1)} all-gather(f32[1,4,512]{2,1,0:T(4,128)S(1)} %maximum_bitcast_fusion), channel_id=3, replica_groups=mesh['dp_0'=4,'dp_1'=4,'dp_2'=2,'tensor'=8] {'dp_0'}, dimensions={0}, use_global_device_ids=true | all-gather | bytes 40960 | tf_op jit(solution)/shard_map/all_gather | solution.py:27
  132.5 11.9 %all-gather.6 = f32[4,4,512]{2,1,0:T(4,128)S(1)} all-gather(f32[1,4,512]{2,1,0:T(4,128)S(1)} %maximum_bitcast_fusion.1), channel_id=4, replica_groups=mesh['dp_0'=4,'dp_1'=4,'dp_2'=2,'tensor'=8] {'dp_1'}, dimensions={0}, use_global_device_ids=true | all-gather | bytes 40960 | tf_op jit(solution)/shard_map/all_gather | solution.py:27
  144.5 1.8 all-gather.7
  146.4 26.0 %all-gather.8 = f32[8,4,512]{2,1,0:T(4,128)S(1)} all-gather(f32[1,4,512]{2,1,0:T(4,128)S(1)} %maximum_bitcast_fusion.3), channel_id=6, replica_groups=mesh['dp_0'=4,'dp_1'=4,'dp_2'=2,'tensor'=8] {'tensor'}, dimensions={0}, use_global_device_ids=true | all-gather | bytes 73728 | tf_op jit(solution)/shard_map/all_gather | solution.py:27
  172.6 0.6 fusion.77
  173.2 0.6 fusion.69
  175.1 0.6 dynamic_slice.7
  175.7 0.5 compare_select_fusion.1
  (39 shorter events, 0.5 us)
Async XLA Ops:
  7.2 2.5 %copy-start = (bf16[16,256,256]{2,1,0:T(8,128)(2,1)S(1)}, bf16[16,256,256]{2,1,0:T(8,128)(2,1)}, u32[]{:S(2)}) copy-start(bf16[16,256,256]{2,1,0:T(8,128)(2,1)} %param.16) | copy-start | bytes 6291460
  7.2 3.5 %copy-start.4 = (bf16[16,256]{1,0:T(8,128)(2,1)S(1)}, bf16[16,256]{1,0:T(8,128)(2,1)}, u32[]{:S(2)}) copy-start(bf16[16,256]{1,0:T(8,128)(2,1)} %param.15) | copy-start | bytes 24580
  7.2 53.7 %all-gather.14.cloned.1.call-start = ((), (), s32[]{:S(2)}) async-start(), calls=%async_computation.1 | async-start | bytes 2654208 | tf_op jit(solution)/shard_map/all_gather | solution.py:16
  16.6 46.2 %copy-start.1 = (bf16[16,4608]{1,0:T(8,128)(2,1)S(1)}, bf16[16,4608]{1,0:T(8,128)(2,1)}, u32[]{:S(2)}) copy-start(bf16[16,4608]{1,0:T(8,128)(2,1)} %param.20) | copy-start | bytes 442372
  16.6 46.2 %copy-start.2 = (f32[4608]{0:T(1024)S(1)}, f32[4608]{0:T(1024)}, u32[]{:S(2)}) copy-start(f32[4608]{0:T(1024)} %param.21) | copy-start | bytes 55300
  16.6 46.5 %copy-start.3 = (f32[4608]{0:T(1024)S(1)}, f32[4608]{0:T(1024)}, u32[]{:S(2)}) copy-start(f32[4608]{0:T(1024)} %param.22) | copy-start | bytes 55300
  16.6 47.3 %copy-start.5 = (s32[16]{0:T(128)S(1)}, s32[16]{0:T(128)}, u32[]{:S(2)}) copy-start(s32[16]{0:T(128)} %param.25) | copy-start | bytes 196
  16.7 48.9 %copy-start.7 = (u32[256]{0:T(256)S(1)}, u32[256]{0:T(256)}, u32[]{:S(2)}) copy-start(u32[256]{0:T(256)} %constant.77) | copy-start | bytes 3076
  16.7 50.1 %copy-start.6 = (s32[16]{0:T(128)S(1)}, s32[16]{0:T(128)}, u32[]{:S(2)}) copy-start(s32[16]{0:T(128)} %param.24) | copy-start | bytes 196
  16.7 97.5 %all-gather.12.cloned.1.call-start = ((), (), s32[]{:S(2)}) async-start(), calls=%async_computation | async-start | bytes 4866048 | tf_op jit(solution)/shard_map/all_gather | solution.py:79
Sparse Core Ops, SparseCore 0:
  16.8 44.0 all-gather.13
  64.0 50.0 all-gather.11
where the time goes:
time: 185 us; the launch traced here: 184 us
  waiting for transfers between devices  75.2 us (41%)
  blocking collectives  67.1 us (36%)
  between operations  18.2 us (10%)
  matrix products  12.6 us (7%)
  other arithmetic  7.08 us (4%)
  local copies, waits for them, and re-layouts  3.94 us (2%)
    all_gather x4, blocking collectives, all_in_one(): both, at, found = (lax.all_gather(jnp.concatenate(lines), axis), 0, {})  51.7 us
    all_gather x1, waiting for transfers between devices, gathered_total(): return lax.all_gather(shard, axis).sum(0)  44.1 us
    all_gather x1, waiting for transfers between devices, collect_slots(): lax.all_gather(hidden, DP, axis=0, tiled=True)  31 us
    unnamed x1, blocking collectives  15.4 us
    dot_general x1, matrix products, on_device(): lax.dot_general(every, vocab_weight, (((1,), (1,)), ((), ())), preferred_...  5.93 us
    dot_general x1, matrix products, on_device(): jnp.dot(attn, out_weight, preferred_element_type=jnp.float32)  3.79 us
  transfers between devices with their start and end apart: 2, of which 2 were waited for; matrix products, arithmetic and copies ran while one was open for 1% of the time, Pallas kernels for 0%

commit v1 on v0

v1 whole, which is shorter than its diff:
```python
import jax
import jax.numpy as jnp
from jax import lax
from jax.sharding import Mesh
from jax.sharding import PartitionSpec as P

D = 4608
HEADS = 32
KV_HEADS = 16
HEAD_DIM = 128
DP = ("dp_0", "dp_1", "dp_2")
DP_TENSOR = ("dp_0", "dp_1", "dp_2", "tensor")
PLANE = ("dp_0", "dp_1")
CHIPS = ("dp_0", "dp_1", "tensor")
META = 128


def attend_local(query, incoming_key, new_value, key_cache, value_cache, cache_len):
    slot_dev = query.shape[0]
    positions = key_cache.shape[1]
    kv_local = incoming_key.shape[1] // HEAD_DIM
    group = HEADS // KV_HEADS
    query_vector = query.reshape(slot_dev, kv_local, group, HEAD_DIM)
    keys = key_cache.reshape(slot_dev, positions, kv_local, HEAD_DIM)
    values = value_cache.reshape(slot_dev, positions, kv_local, HEAD_DIM)
    self_key = incoming_key.reshape(slot_dev, kv_local, HEAD_DIM)
    own_value = new_value.reshape(slot_dev, kv_local, HEAD_DIM).astype(jnp.float32)
    scores = (
        jnp.einsum("bkgd,bckd->bkgc", query_vector, keys, preferred_element_type=jnp.float32) / 12.0
    )
    self_entry = (
        jnp.einsum("qyxm,qym->qyx", query_vector, self_key, preferred_element_type=jnp.float32)
        / 12.0
    )
    valid = (
        jnp.arange(positions, dtype=jnp.int32)[None, None, None, :] < cache_len[:, None, None, None]
    )
    scores = jnp.where(valid, scores, -1e30)
    top = jnp.maximum(jnp.max(scores, axis=-1), self_entry)
    expo = jnp.where(valid, jnp.exp(scores - top[..., None]), 0.0)
    own_exp = jnp.exp(self_entry - top)
    total = jnp.sum(expo, axis=-1) + own_exp
    weight = (expo / total[..., None]).astype(jnp.bfloat16)
    own_weight = (own_exp / total).astype(jnp.bfloat16).astype(jnp.float32)
    attn = jnp.einsum("bkgc,bckd->bkgd", weight, values, preferred_element_type=jnp.float32)
    attn = attn + own_weight[..., None] * own_value[:, :, None, :]
    return attn.astype(jnp.bfloat16).reshape(slot_dev, kv_local * group * HEAD_DIM)


def exchange(blocks, axes):
    return lax.all_to_all(blocks, axes, 0, 0, tiled=True)


def spread(block, axes):
    count = 1
    for axis in axes if isinstance(axes, tuple) else (axes,):
        count *= lax.axis_size(axis)
    return exchange(jnp.broadcast_to(block[None], (count, *block.shape)), axes)


def other_core(value):
    return lax.ppermute(value, "dp_2", [(0, 1), (1, 0)])


def inverse_rms(rows):
    return lax.rsqrt(jnp.mean(rows * rows, axis=-1, keepdims=True) + 1e-06)


def vocab_part(every, ids, rows, start):
    logits = lax.dot_general(
        every, rows, (((1,), (1,)), ((), ())), preferred_element_type=jnp.float32
    )
    hit = jnp.arange(rows.shape[0], dtype=jnp.int32)[None, :] == (ids - start)[:, None]
    picked = jnp.sum(jnp.where(hit, logits, 0.0), axis=1)
    top = jnp.max(logits, axis=1)
    total = jnp.sum(jnp.exp(logits - top[:, None]), axis=1)
    return top, total, picked


def on_device(
    query,
    incoming_key,
    new_value,
    key_cache,
    value_cache,
    cache_len,
    out_weight,
    residual,
    post_gain,
    final_gain,
    vocab_weight,
    sampled,
    stop_flag,
):
    slot_dev = query.shape[0]
    nz = lax.axis_size("tensor")
    z = lax.axis_index("tensor")
    core = lax.axis_index("dp_2")
    plane = lax.axis_index(PLANE)
    planes = lax.axis_size(PLANE)
    freed = (stop_flag == 1).astype(jnp.int32)
    count = jnp.sum(freed)

    vocab_other = other_core(vocab_weight)
    count_other = other_core(jnp.broadcast_to(count.astype(jnp.float32), (8, 128)))[0, 0]

    attn = attend_local(query, incoming_key, new_value, key_cache, value_cache, cache_len)
    partial_value = jnp.dot(attn, out_weight, preferred_element_type=jnp.float32)
    per = slot_dev // nz
    pieces = exchange(partial_value.astype(jnp.bfloat16).reshape(nz, per, D), "tensor")
    proj = jnp.sum(pieces.astype(jnp.float32), axis=0)
    post = proj * inverse_rms(proj) * post_gain
    own_residual = lax.dynamic_slice_in_dim(residual, z * per, per, 0)
    mix = (own_residual.astype(jnp.float32) + post).astype(jnp.bfloat16)
    full_mix = spread(mix, "tensor").reshape(slot_dev, D)
    mixed = full_mix.astype(jnp.float32)
    hidden = (mixed * inverse_rms(mixed) * final_gain).astype(jnp.bfloat16)
    width = D // nz
    new_residual = lax.dynamic_slice_in_dim(full_mix, z * width, width, 1)

    meta = jnp.stack(
        [
            sampled & 63,
            (sampled >> 6) & 63,
            sampled >> 12,
            freed,
            jnp.broadcast_to(count_other.astype(jnp.int32), (slot_dev,)),
        ],
        axis=1,
    ).astype(jnp.bfloat16)
    meta = jnp.pad(meta, ((0, 0), (0, META - meta.shape[1])))
    every = spread(jnp.concatenate([hidden, meta], axis=1), PLANE)
    every = every.reshape(planes * slot_dev, D + META)
    notes = every[:, D : D + 5].astype(jnp.int32)
    ids = notes[:, 0] + notes[:, 1] * 64 + notes[:, 2] * 4096
    every = every[:, :D]

    per_device = vocab_weight.shape[0]
    start = (lax.axis_index(DP) * nz + z) * per_device
    start_other = ((plane * 2 + 1 - core) * nz + z) * per_device
    top_a, sum_a, picked_a = vocab_part(every, ids, vocab_weight, start)
    top_b, sum_b, picked_b = vocab_part(every, ids, vocab_other, start_other)
    top = jnp.maximum(top_a, top_b)
    total = sum_a * jnp.exp(top_a - top) + sum_b * jnp.exp(top_b - top)
    pair = jnp.stack([top + jnp.log(total), picked_a + picked_b], axis=0)
    pair = pair.reshape(2, planes, slot_dev).transpose(1, 0, 2).reshape(planes, 1, 2 * slot_dev)
    pair = jnp.broadcast_to(pair, (planes, nz, 2 * slot_dev)).reshape(planes * nz, 2 * slot_dev)
    gathered = exchange(pair, CHIPS)
    parts = gathered[:, :slot_dev]
    highest = jnp.max(parts, axis=0)
    overall = jnp.log(jnp.sum(jnp.exp(parts - highest[None]), axis=0)) + highest
    token_logprob = jnp.sum(gathered[:, slot_dev:], axis=0) - overall

    flags = notes[:, 3].reshape(planes, slot_dev)
    counts_here = jnp.sum(flags, axis=1)
    counts_there = notes[:, 4].reshape(planes, slot_dev)[:, 0]
    chips = jnp.arange(planes, dtype=jnp.int32)
    both = counts_here + counts_there
    before = jnp.sum(jnp.where(chips < plane, both, 0))
    before = before + jnp.where(core == 1, count_other.astype(jnp.int32), 0)
    released = jnp.sum(both).astype(jnp.int32)
    insert_rank = jnp.where(freed == 1, jnp.cumsum(freed) - freed + before, -1)
    return (new_residual, token_logprob, insert_rank.astype(jnp.int32), released)


def solution(mesh):
    split = Mesh(
        mesh.devices.reshape(4, 4, 2, mesh.shape["tensor"]), ("dp_0", "dp_1", "dp_2", "tensor")
    )
    in_specs = (
        P(DP, "tensor"),
        P(DP, "tensor"),
        P(DP, "tensor"),
        P(DP, None, "tensor"),
        P(DP, None, "tensor"),
        P(DP),
        P("tensor", None),
        P(DP, None),
        P(),
        P(),
        P(DP_TENSOR, None),
        P(DP),
        P(DP),
    )
    out_specs = (P(DP, "tensor"), P(DP), P(DP), P())
    return jax.shard_map(
        on_device, mesh=split, in_specs=in_specs, out_specs=out_specs, check_vma=False
    )
```

time: 185 us -> 115 us (0.62)
  blocking collectives: 67.1 us -> 0 us
  starting transfers between devices: 0.08 us -> 27.2 us
  waiting for transfers between devices: 75.2 us -> 54.7 us
  between operations: 18.2 us -> 2.88 us
  local copies, waits for them, and re-layouts: 3.94 us -> 7.65 us
  matrix products: 12.6 us -> 15.1 us
    all_gather x2 -> x0, waiting for transfers between devices: 75.1 us -> none  [the longest x1 44.1 us: gathered_total(): return lax.all_gather(shard, axis).sum(0)]
    all_to_all x0 -> x4, waiting for transfers between devices: none -> 54.7 us  [exchange(): return lax.all_to_all(blocks, axes, 0, 0, tiled=True)]
    all_gather x4 -> x0, blocking collectives: 51.7 us -> none  [all_in_one(): both, at, found = (lax.all_gather(jnp.concatenate(lines), axis), 0, {})]
    all_to_all x0 -> x4, starting transfers between devices: none -> 26.6 us  [exchange(): return lax.all_to_all(blocks, axes, 0, 0, tiled=True)]
    unnamed x1 -> x0, blocking collectives: 15.4 us -> none
    dot_general x1 -> x2, matrix products: 5.93 us -> 9.09 us  [vocab_part(): lax.dot_general(every, rows, (((1,), (1,)), ((), ())), preferred_element_...]
    broadcast_in_dim x0 -> x5, local copies, waits for them, and re-layouts: none -> 3.1 us  [the longest x2 2.39 us: spread(): return exchange(jnp.broadcast_to(block[None], (count, *block.shape)), axes)]
    reduce_sum x6 -> x7, other arithmetic: 3.71 us -> 1.88 us  [the longest x1 0.65 us: on_device(): released = jnp.sum(both).astype(jnp.int32)]
  transfers between devices with their start and end apart: 2 -> 6, of which waited for: 2 -> 4; matrix products, arithmetic and copies ran while one was open for 1% -> 12% of each run, Pallas kernels for 0% -> 0%
where the time goes in v1:
time: 115 us
  waiting for transfers between devices  54.7 us (48%)
  starting transfers between devices  27.2 us (24%)
  matrix products  15.1 us (13%)
  local copies, waits for them, and re-layouts  7.65 us (7%)
  other arithmetic  7.32 us (6%)
  between operations  2.88 us (3%)
    all_to_all x4, waiting for transfers between devices, exchange(): return lax.all_to_all(blocks, axes, 0, 0, tiled=True)  54.7 us
    all_to_all x4, starting transfers between devices, exchange(): return lax.all_to_all(blocks, axes, 0, 0, tiled=True)  26.6 us
    dot_general x2, matrix products, vocab_part(): lax.dot_general(every, rows, (((1,), (1,)), ((), ())), preferred_element_...  9.09 us
    dot_general x1, matrix products, on_device(): jnp.dot(attn, out_weight, preferred_element_type=jnp.float32)  3.07 us
    broadcast_in_dim x2, local copies, waits for them, and re-layouts, spread(): return exchange(jnp.broadcast_to(block[None], (count, *block.shape)), axes)  2.39 us
  transfers between devices with their start and end apart: 6, of which 4 were waited for; matrix products, arithmetic and copies ran while one was open for 12% of the time, Pallas kernels for 0%

profile of v1, /device:TPU:8, one launch (start us, length us, event | category | flops | bytes accessed | tf_op | source)
XLA Modules:
  0.0 114.8 jit_solution(17121386958418873205)
XLA Ops:
  0.6 0.0 copy-start
  0.6 0.0 copy-start.3
  0.7 0.9 iota_compare_fusion.3
  1.5 0.7 reshape.224
  2.3 0.7 reshape.237
  3.0 0.1 fusion.40
  3.1 0.0 copy-done
  3.1 0.7 fusion.37
  3.9 0.2 fusion.27
  4.2 0.0 copy-done.3
  4.2 2.0 %fusion.19 = bf16[16,2,2,128]{3,2,1,0:T(2,128)(2,1)S(1)} fusion(f32[16,2,2]{2,1,0:T(2,128)S(1)} %get-tuple-element.17, f32[16,2,128]{2,1,0:T(2,128)S(1)} %reshape.233, f32[16,2,2]{2,1,0:T(2,128)S(1)} %get-tuple-element.16, f32[16,2,2,256]{3,2,1,0:T(2,128)S(1)} %get-tuple-element.24, pred[16,256]{1,0:T(8,128)(4,1)S(1)} %iota_compare_fusion.3, ...), kind=kOutput, calls=%fused_computation.14 | convolution fusion | flops 4284416 | bytes 2200320 | tf_op jit(solution)/shard_map/bkgc,bckd->bkgd/dot_general | solution.py:45
  6.3 0.0 copy-start.5
  6.3 0.0 copy-start.2
  6.3 0.0 copy-start.4
  6.3 0.0 copy-start.1
  6.3 3.1 %convolution_convert_fusion = bf16[16,4608]{1,0:T(8,128)(2,1)S(1)} fusion(bf16[16,512]{1,0:T(8,128)(2,1)S(1)} %reshape.228, bf16[512,4608]{1,0:T(8,128)(2,1)} %param.19), kind=kOutput, calls=%fused_computation | convolution fusion | flops 75571200 | bytes 4882432 | tf_op jit(solution)/shard_map/dot_general | solution.py:108
  9.4 0.7 reshape.229
  10.1 8.5 %all-to-all-start = ((bf16[8,2,4608]{2,1,0:T(2,128)(2,1)}), bf16[8,2,4608]{2,1,0:T(2,128)(2,1)S(1)}, u32[]{:S(2)}, u32[]{:S(2)}) async-start(bf16[8,2,4608]{2,1,0:T(2,128)(2,1)} %reshape.229), calls=%async_computation | async-start | bytes 294912 | tf_op jit(solution)/shard_map/all_to_all | solution.py:51
  18.6 0.6 fusion.32
  19.9 0.1 collective-permute-start
  20.0 0.5 collective-permute-start.1
  20.5 7.5 %all-to-all-done = bf16[8,2,4608]{2,1,0:T(2,128)(2,1)S(1)} async-done(((bf16[8,2,4608]{2,1,0:T(2,128)(2,1)}), bf16[8,2,4608]{2,1,0:T(2,128)(2,1)S(1)}, u32[]{:S(2)}, u32[]{:S(2)}) %all-to-all-start) | async-done | bytes 147488 | tf_op jit(solution)/shard_map/all_to_all | solution.py:51
  28.0 0.1 convert_reduce_fusion
  28.1 0.2 multiply_reduce_fusion.1
  28.3 1.0 add_convert_fusion
  29.3 0.8 broadcast_in_dim.72
  30.0 3.4 %all-to-all-start.1 = ((bf16[8,2,4608]{2,1,0:T(2,128)(2,1)}), bf16[8,2,4608]{2,1,0:T(2,128)(2,1)S(1)}, u32[]{:S(2)}, u32[]{:S(2)}) async-start(bf16[8,2,4608]{2,1,0:T(2,128)(2,1)} %broadcast_in_dim.72), calls=%async_computation.1 | async-start | bytes 294912 | tf_op jit(solution)/shard_map/all_to_all | solution.py:51
  33.5 0.0 collective-permute-done
  33.5 0.5 slice.33
  34.7 0.1 copy.36
  34.8 7.8 %all-to-all-done.1 = bf16[8,2,4608]{2,1,0:T(2,128)(2,1)S(1)} async-done(((bf16[8,2,4608]{2,1,0:T(2,128)(2,1)}), bf16[8,2,4608]{2,1,0:T(2,128)(2,1)S(1)}, u32[]{:S(2)}, u32[]{:S(2)}) %all-to-all-start.1) | async-done | bytes 147488 | tf_op jit(solution)/shard_map/all_to_all | solution.py:51
  42.6 0.2 multiply_reduce_fusion
  42.8 0.1 rsqrt.21
  42.9 0.1 reshape.230
  43.0 0.1 multiply_convert_fusion
  43.1 1.6 %broadcast_in_dim.74 = bf16[16,16,4736]{2,1,0:T(8,128)(2,1)} broadcast(bf16[16,4736]{1,0:T(8,128)(2,1)S(1)} %fusion.23), dimensions={1,2} | broadcast | bytes 2576384 | tf_op jit(solution)/shard_map/broadcast_in_dim | solution.py:58
  44.8 7.4 %all-to-all-start.2 = ((bf16[16,16,4736]{2,1,0:T(8,128)(2,1)}), bf16[16,16,4736]{2,1,0:T(8,128)(2,1)}, u32[]{:S(2)}, u32[]{:S(2)}) async-start(bf16[16,16,4736]{2,1,0:T(8,128)(2,1)} %broadcast_in_dim.74), calls=%async_computation.2 | async-start | bytes 4849664 | tf_op jit(solution)/shard_map/all_to_all | solution.py:51
  52.2 0.1 copy.33
  52.3 0.1 reduce.3
  52.4 0.7 constant_dynamic-slice_fusion
  53.1 28.9 %all-to-all-done.2 = bf16[16,16,4736]{2,1,0:T(8,128)(2,1)} async-done(((bf16[16,16,4736]{2,1,0:T(8,128)(2,1)}), bf16[16,16,4736]{2,1,0:T(8,128)(2,1)}, u32[]{:S(2)}, u32[]{:S(2)}) %all-to-all-start.2) | async-done | bytes 2424864 | tf_op jit(solution)/shard_map/all_to_all | solution.py:51
  81.9 4.5 %fusion.38 = (f32[256]{0:T(256)S(1)}, f32[256,512]{1,0:T(8,128)S(1)}) fusion(bf16[512,4608]{1,0:T(8,128)(2,1)} %param.23, bf16[256,4736]{1,0:T(8,128)(2,1)} %bitcast.7), kind=kOutput, calls=%fused_computation.74 | convolution fusion | flops 1208090368 | bytes 7603200 | tf_op jit(solution)/shard_map/dot_general | solution.py:70
  86.5 0.1 reduce_max.42
  86.6 0.9 slice_convert_fusion
  87.4 0.4 slice_reduce_fusion
  87.8 0.1 reshape_squeeze.6
  87.9 0.1 reduce_sum.143
  88.0 0.1 reshape_squeeze.7
  88.1 0.1 slice_reduce_fusion.4
  88.2 0.6 add_reduce_fusion
  89.5 0.0 collective-permute-done.1
  89.5 4.5 %fusion.39 = (f32[256]{0:T(256)S(1)}, f32[256,512]{1,0:T(8,128)S(1)}) fusion(bf16[512,4608]{1,0:T(8,128)(2,1)} %collective-permute-done.1, bf16[256,4736]{1,0:T(8,128)(2,1)} %bitcast.7), kind=kOutput, calls=%fused_computation.75 | convolution fusion | flops 1208090368 | bytes 7603200 | tf_op jit(solution)/shard_map/dot_general | solution.py:70
  94.1 0.1 reduce_max.44
  94.2 0.5 exponential_reduce_fusion
  94.7 0.1 reduce_sum.138
  94.8 0.1 reduce_sum.136
  94.9 0.1 add.131
  95.0 0.1 broadcast_in_dim.76
  95.1 0.6 broadcast_in_dim.77
  95.7 7.3 %all-to-all-start.3 = ((f32[128,1,32]{2,1,0:T(1,128)}), f32[128,1,32]{2,1,0:T(1,128)S(1)}, u32[]{:S(2)}, u32[]{:S(2)}) async-start(f32[128,1,32]{2,1,0:T(1,128)} %bitcast.9), calls=%async_computation.3 | async-start | bytes 131072 | tf_op jit(solution)/shard_map/all_to_all | solution.py:51
  103.1 0.5 compare_select_fusion.1
  103.6 10.6 %all-to-all-done.3 = f32[128,1,32]{2,1,0:T(1,128)S(1)} async-done(((f32[128,1,32]{2,1,0:T(1,128)}), f32[128,1,32]{2,1,0:T(1,128)S(1)}, u32[]{:S(2)}, u32[]{:S(2)}) %all-to-all-start.3) | async-done | bytes 16416 | tf_op jit(solution)/shard_map/all_to_all | solution.py:51
  114.2 0.1 exponential_reduce_fusion.2
  114.3 0.5 add_subtract_fusion
  (21 shorter events, 0.3 us)
Async XLA Ops:
  0.6 2.5 %copy-start = (bf16[16,256,256]{2,1,0:T(8,128)(2,1)S(1)}, bf16[16,256,256]{2,1,0:T(8,128)(2,1)}, u32[]{:S(2)}) copy-start(bf16[16,256,256]{2,1,0:T(8,128)(2,1)} %param.16) | copy-start | bytes 6291460
  0.6 3.5 %copy-start.3 = (bf16[16,256]{1,0:T(8,128)(2,1)S(1)}, bf16[16,256]{1,0:T(8,128)(2,1)}, u32[]{:S(2)}) copy-start(bf16[16,256]{1,0:T(8,128)(2,1)} %param.15) | copy-start | bytes 24580
  6.3 12.3 %copy-start.5 = (s32[16]{0:T(128)S(1)}, s32[16]{0:T(128)}, u32[]{:S(2)}) copy-start(s32[16]{0:T(128)} %param.25) | copy-start | bytes 196
  6.3 22.0 %copy-start.2 = (f32[4608]{0:T(1024)S(1)}, f32[4608]{0:T(1024)}, u32[]{:S(2)}) copy-start(f32[4608]{0:T(1024)} %param.21) | copy-start | bytes 55300
  6.3 27.1 %copy-start.4 = (s32[16]{0:T(128)S(1)}, s32[16]{0:T(128)}, u32[]{:S(2)}) copy-start(s32[16]{0:T(128)} %param.24) | copy-start | bytes 196
  6.3 36.7 %copy-start.1 = (f32[4608]{0:T(1024)S(1)}, f32[4608]{0:T(1024)}, u32[]{:S(2)}) copy-start(f32[4608]{0:T(1024)} %param.22) | copy-start | bytes 55300
  10.1 17.9 %all-to-all-start = ((bf16[8,2,4608]{2,1,0:T(2,128)(2,1)}), bf16[8,2,4608]{2,1,0:T(2,128)(2,1)S(1)}, u32[]{:S(2)}, u32[]{:S(2)}) async-start(bf16[8,2,4608]{2,1,0:T(2,128)(2,1)} %reshape.229), calls=%async_computation | async-start | bytes 294912 | tf_op jit(solution)/shard_map/all_to_all | solution.py:51
  19.9 13.6 %collective-permute-start = (f32[8,128]{1,0:T(8,128)S(1)}, f32[8,128]{1,0:T(8,128)S(1)}, u32[]{:S(2)}, u32[]{:S(2)}) collective-permute-start(f32[8,128]{1,0:T(8,128)S(1)} %broadcast_in_dim.73), channel_id=1, source_target_pairs={{0,8},{8,0},{1,9},{9,1},{2,10},{10,2},{3,11},{11,3},{4,12},{12,4},... | collective-permute-start | bytes 12296 | tf_op jit(solution)/shard_map/ppermute | solution.py:62
  20.0 69.6 %collective-permute-start.1 = (bf16[512,4608]{1,0:T(8,128)(2,1)}, bf16[512,4608]{1,0:T(8,128)(2,1)}, u32[]{:S(2)}, u32[]{:S(2)}) collective-permute-start(bf16[512,4608]{1,0:T(8,128)(2,1)} %param.23), channel_id=1, source_target_pairs={{0,8},{8,0},{1,9},{9,1},{2,10},{10,2},{3,11},{11,3},{4,12},{12,4},... | collective-permute-start | bytes 14155784 | tf_op jit(solution)/shard_map/ppermute | solution.py:62
  30.0 12.5 %all-to-all-start.1 = ((bf16[8,2,4608]{2,1,0:T(2,128)(2,1)}), bf16[8,2,4608]{2,1,0:T(2,128)(2,1)S(1)}, u32[]{:S(2)}, u32[]{:S(2)}) async-start(bf16[8,2,4608]{2,1,0:T(2,128)(2,1)} %broadcast_in_dim.72), calls=%async_computation.1 | async-start | bytes 294912 | tf_op jit(solution)/shard_map/all_to_all | solution.py:51
  44.8 37.2 %all-to-all-start.2 = ((bf16[16,16,4736]{2,1,0:T(8,128)(2,1)}), bf16[16,16,4736]{2,1,0:T(8,128)(2,1)}, u32[]{:S(2)}, u32[]{:S(2)}) async-start(bf16[16,16,4736]{2,1,0:T(8,128)(2,1)} %broadcast_in_dim.74), calls=%async_computation.2 | async-start | bytes 4849664 | tf_op jit(solution)/shard_map/all_to_all | solution.py:51
  95.7 18.4 %all-to-all-start.3 = ((f32[128,1,32]{2,1,0:T(1,128)}), f32[128,1,32]{2,1,0:T(1,128)S(1)}, u32[]{:S(2)}, u32[]{:S(2)}) async-start(f32[128,1,32]{2,1,0:T(1,128)} %bitcast.9), calls=%async_computation.3 | async-start | bytes 131072 | tf_op jit(solution)/shard_map/all_to_all | solution.py:51

commit v2 on v1

--- a/solution.py
+++ b/solution.py
@@ -1,6 +1,8 @@
 import jax
 import jax.numpy as jnp
 from jax import lax
+from jax.experimental import pallas as pl
+from jax.experimental.pallas import tpu as pltpu
 from jax.sharding import Mesh
 from jax.sharding import PartitionSpec as P
 
@@ -13,6 +15,9 @@
 PLANE = ("dp_0", "dp_1")
 CHIPS = ("dp_0", "dp_1", "tensor")
 META = 128
+TILE = 256
+VMEM_GRANT = 60 * 1024 * 1024
+LAST_GRANT = 60 * 1024 * 1024
 
 
 def attend_local(query, incoming_key, new_value, key_cache, value_cache, cache_len):
@@ -66,15 +71,139 @@
     return lax.rsqrt(jnp.mean(rows * rows, axis=-1, keepdims=True) + 1e-06)
 
 
-def vocab_part(every, ids, rows, start):
-    logits = lax.dot_general(
-        every, rows, (((1,), (1,)), ((), ())), preferred_element_type=jnp.float32
-    )
-    hit = jnp.arange(rows.shape[0], dtype=jnp.int32)[None, :] == (ids - start)[:, None]
-    picked = jnp.sum(jnp.where(hit, logits, 0.0), axis=1)
-    top = jnp.max(logits, axis=1)
-    total = jnp.sum(jnp.exp(logits - top[:, None]), axis=1)
-    return top, total, picked
+def product(rows, slots):
+    return lax.dot_general(
+        rows, slots, (((1,), (1,)), ((), ())), preferred_element_type=jnp.float32
+    )
+
+
+def load_rows(own_hbm, other_hbm, column, width, weights, sems):
+    copies = []
+    for which, source in enumerate((own_hbm, other_hbm)):
+        for tile in range(own_hbm.shape[0] // TILE):
+            place = which * (own_hbm.shape[0] // TILE) + tile
+            copy = pltpu.make_async_copy(
+                source.at[pl.ds(tile * TILE, TILE), pl.ds(column, width)],
+                weights.at[place],
+                sems.at[place],
+            )
+            copy.start()
+            copies.append(copy)
+    return copies
+
+
+def first_half_kernel(every_hbm, own_hbm, other_hbm, part_hbm, every, weights, part, in_sem, out_sem, sems):
+    width = every.shape[1]
+    load = pltpu.make_async_copy(every_hbm, every, in_sem)
+    load.start()
+    copies = load_rows(own_hbm, other_hbm, 0, width, weights, sems)
+    load.wait()
+    stores = []
+    for place, copy in enumerate(copies):
+        copy.wait()
+        part[place] = product(weights[place], every[...])
+        store = pltpu.make_async_copy(part.at[place], part_hbm.at[place], out_sem.at[place])
+        store.start()
+        stores.append(store)
+    for store in stores:
+        store.wait()
+
+
+def first_half(every, own, other):
+    slots, width = every.shape
+    rows = own.shape[0]
+    tiles = 2 * rows // TILE
+    hbm = pl.BlockSpec(memory_space=pltpu.HBM)
+    return pl.pallas_call(
+        first_half_kernel,
+        in_specs=[hbm, hbm, hbm],
+        out_specs=hbm,
+        out_shape=jax.ShapeDtypeStruct((tiles, TILE, slots), jnp.float32),
+        scratch_shapes=[
+            pltpu.VMEM((slots, width), jnp.bfloat16),
+            pltpu.VMEM((tiles, TILE, width), jnp.bfloat16),
+            pltpu.VMEM((tiles, TILE, slots), jnp.float32),
+            pltpu.SemaphoreType.DMA,
+            pltpu.SemaphoreType.DMA((tiles,)),
+            pltpu.SemaphoreType.DMA((tiles,)),
+        ],
+        compiler_params=pltpu.CompilerParams(vmem_limit_bytes=VMEM_GRANT),
+        cost_estimate=pl.CostEstimate(
+            flops=4 * rows * slots * width, bytes_accessed=4 * rows * width, transcendentals=0
+        ),
+        name="first_half",
+    )(every, own, other)
+
+
+def second_half_kernel(
+    starts_ref, every_hbm, own_hbm, other_hbm, part_hbm, out_ref, every, weights, part, in_sem, sems, part_sems
+):
+    tiles, _, width = weights.shape
+    half_tiles = tiles // 2
+    slots = every.shape[0]
+    load = pltpu.make_async_copy(every_hbm, every, in_sem)
+    load.start()
+    copies = load_rows(own_hbm, other_hbm, width, width, weights, sems)
+    parts = []
+    for place in range(tiles):
+        copy = pltpu.make_async_copy(part_hbm.at[place], part.at[place], part_sems.at[place])
+        copy.start()
+        parts.append(copy)
+    load.wait()
+    lane = lax.broadcasted_iota(jnp.int32, (16, META), 1)
+    row = lax.broadcasted_iota(jnp.int32, (16, META), 0)
+    digit = jnp.where(lane == 0, 1.0, jnp.where(lane == 1, 64.0, jnp.where(lane == 2, 4096.0, 0.0)))
+    pick = jnp.where(row == 0, digit, jnp.where(lane == row + 2, 1.0, 0.0))
+    notes = product(pick.astype(jnp.bfloat16), every[:, width:])
+    ids = notes[0:1, :].astype(jnp.int32)
+    line = lax.broadcasted_iota(jnp.int32, (TILE, slots), 0)
+    top = jnp.full((1, slots), -jnp.inf, jnp.float32)
+    total = jnp.zeros((1, slots), jnp.float32)
+    picked = jnp.zeros((1, slots), jnp.float32)
+    for place in range(tiles):
+        copies[place].wait()
+        parts[place].wait()
+        logits = part[place] + product(weights[place], every[:, :width])
+        part[place] = logits
+        begin = starts_ref[place // half_tiles] + (place % half_tiles) * TILE
+        picked = picked + jnp.sum(jnp.where(line == ids - begin, logits, 0.0), axis=0, keepdims=True)
+        higher = jnp.maximum(top, jnp.max(logits, axis=0, keepdims=True))
+        total = total * jnp.exp(top - higher) + jnp.sum(
+            jnp.exp(logits - higher), axis=0, keepdims=True
+        )
+        top = higher
+    out_ref[0:1, :] = top + jnp.log(total)
+    out_ref[1:2, :] = picked
+    out_ref[2:8, :] = notes[1:7, :]
+
+
+def second_half(starts, every, own, other, part):
+    slots, wide = every.shape
+    width = wide - META
+    rows = own.shape[0]
+    tiles = 2 * rows // TILE
+    hbm = pl.BlockSpec(memory_space=pltpu.HBM)
+    return pl.pallas_call(
+        second_half_kernel,
+        in_specs=[pl.BlockSpec(memory_space=pltpu.SMEM), hbm, hbm, hbm, hbm],
+        out_specs=pl.BlockSpec(memory_space=pltpu.VMEM),
+        out_shape=jax.ShapeDtypeStruct((8, slots), jnp.float32),
+        scratch_shapes=[
+            pltpu.VMEM((slots, wide), jnp.bfloat16),
+            pltpu.VMEM((tiles, TILE, width), jnp.bfloat16),
+            pltpu.VMEM((tiles, TILE, slots), jnp.float32),
+            pltpu.SemaphoreType.DMA,
+            pltpu.SemaphoreType.DMA((tiles,)),
+            pltpu.SemaphoreType.DMA((tiles,)),
+        ],
+        compiler_params=pltpu.CompilerParams(vmem_limit_bytes=LAST_GRANT),
+        cost_estimate=pl.CostEstimate(
+            flops=4 * rows * slots * width,
+            bytes_accessed=4 * rows * width,
+            transcendentals=2 * rows * slots,
+        ),
+        name="second_half",
+    )(starts, every, own, other, part)
 
 
 def on_device(
@@ -129,21 +258,20 @@
         axis=1,
     ).astype(jnp.bfloat16)
     meta = jnp.pad(meta, ((0, 0), (0, META - meta.shape[1])))
-    every = spread(jnp.concatenate([hidden, meta], axis=1), PLANE)
-    every = every.reshape(planes * slot_dev, D + META)
-    notes = every[:, D : D + 5].astype(jnp.int32)
-    ids = notes[:, 0] + notes[:, 1] * 64 + notes[:, 2] * 4096
-    every = every[:, :D]
+    half = D // 2
+    slots = planes * slot_dev
+    every_a = spread(hidden[:, :half], PLANE).reshape(slots, half)
+    every_b = spread(jnp.concatenate([hidden[:, half:], meta], axis=1), PLANE)
+    every_b = every_b.reshape(slots, half + META)
 
     per_device = vocab_weight.shape[0]
     start = (lax.axis_index(DP) * nz + z) * per_device
     start_other = ((plane * 2 + 1 - core) * nz + z) * per_device
-    top_a, sum_a, picked_a = vocab_part(every, ids, vocab_weight, start)
-    top_b, sum_b, picked_b = vocab_part(every, ids, vocab_other, start_other)
-    top = jnp.maximum(top_a, top_b)
-    total = sum_a * jnp.exp(top_a - top) + sum_b * jnp.exp(top_b - top)
-    pair = jnp.stack([top + jnp.log(total), picked_a + picked_b], axis=0)
-    pair = pair.reshape(2, planes, slot_dev).transpose(1, 0, 2).reshape(planes, 1, 2 * slot_dev)
+    part = first_half(every_a, vocab_weight, vocab_other)
+    stats = second_half(
+        jnp.stack([start, start_other]), every_b, vocab_weight, vocab_other, part
+    )
+    pair = stats[:2].reshape(2, planes, slot_dev).transpose(1, 0, 2).reshape(planes, 1, 2 * slot_dev)
     pair = jnp.broadcast_to(pair, (planes, nz, 2 * slot_dev)).reshape(planes * nz, 2 * slot_dev)
     gathered = exchange(pair, CHIPS)
     parts = gathered[:, :slot_dev]
@@ -151,9 +279,9 @@
     overall = jnp.log(jnp.sum(jnp.exp(parts - highest[None]), axis=0)) + highest
     token_logprob = jnp.sum(gathered[:, slot_dev:], axis=0) - overall
 
-    flags = notes[:, 3].reshape(planes, slot_dev)
-    counts_here = jnp.sum(flags, axis=1)
-    counts_there = notes[:, 4].reshape(planes, slot_dev)[:, 0]
+    notes = stats[2:4].astype(jnp.int32).reshape(2, planes, slot_dev)
+    counts_here = jnp.sum(notes[0], axis=1)
+    counts_there = notes[1][:, 0]
     chips = jnp.arange(planes, dtype=jnp.int32)
     both = counts_here + counts_there
     before = jnp.sum(jnp.where(chips < plane, both, 0))

time: 115 us -> 117 us (1.017)
  waiting for transfers between devices: 54.7 us -> 38.1 us
  Pallas kernels: 0 us -> 13.8 us
  blocking collectives: 0 us -> 11.6 us
  matrix products: 15.1 us -> 4.39 us
  local copies, waits for them, and re-layouts: 7.65 us -> 10.3 us
    all_to_all x4, waiting for transfers between devices: 54.7 us -> 37 us  [exchange(): return lax.all_to_all(blocks, axes, 0, 0, tiled=True)]
    pallas_call x0 -> x2, Pallas kernels: none -> 13.8 us  [the longest x1 7.54 us: second_half(): pl.pallas_call(second_half_kernel, in_specs=[pl.BlockSpec(memory_space=pl...]
    all_to_all x0 -> x1, blocking collectives: none -> 11.6 us  [exchange(): return lax.all_to_all(blocks, axes, 0, 0, tiled=True)]
    dot_general x2 -> x0, matrix products: 9.09 us -> none  [vocab_part(): lax.dot_general(every, rows, (((1,), (1,)), ((), ())), preferred_element_...]
    unnamed x13 -> x18, local copies, waits for them, and re-layouts: 0.14 us -> 1.9 us
    dot_general x1, matrix products: 2.04 us -> 0.44 us  [attend_local(): jnp.einsum('bkgc,bckd->bkgd', weight, values, preferred_element_type=jnp....]
    broadcast_in_dim x2 -> x3, local copies, waits for them, and re-layouts: 2.39 us -> 2.44 us  [spread(): return exchange(jnp.broadcast_to(block[None], (count, *block.shape)), axes)]
  transfers between devices with their start and end apart: 6 -> 6, of which waited for: 4 -> 5; matrix products, arithmetic and copies ran while one was open for 12% -> 8% of each run, Pallas kernels for 0% -> 5%
where the time goes in v2:
time: 117 us; the launch traced here: 116 us
  waiting for transfers between devices  38.1 us (33%)
  starting transfers between devices  27.5 us (24%)
  Pallas kernels  13.8 us (12%)
  blocking collectives  11.6 us (10%)
  local copies, waits for them, and re-layouts  10.3 us (9%)
  other arithmetic  7.77 us (7%)
  matrix products  4.39 us (4%)
  between operations  2.83 us (2%)
    all_to_all x4, waiting for transfers between devices, exchange(): return lax.all_to_all(blocks, axes, 0, 0, tiled=True)  37 us
    all_to_all x4, starting transfers between devices, exchange(): return lax.all_to_all(blocks, axes, 0, 0, tiled=True)  27.4 us
    all_to_all x1, blocking collectives, exchange(): return lax.all_to_all(blocks, axes, 0, 0, tiled=True)  11.6 us
    pallas_call x1, Pallas kernels, second_half(): pl.pallas_call(second_half_kernel, in_specs=[pl.BlockSpec(memory_space=pl...  7.54 us
    pallas_call x1, Pallas kernels, first_half(): pl.pallas_call(first_half_kernel, in_specs=[hbm, hbm, hbm], out_specs=hbm...  6.28 us
    dot_general x1, matrix products, on_device(): jnp.dot(attn, out_weight, preferred_element_type=jnp.float32)  3.07 us
    broadcast_in_dim x3, local copies, waits for them, and re-layouts, spread(): return exchange(jnp.broadcast_to(block[None], (count, *block.shape)), axes)  2.44 us
  transfers between devices with their start and end apart: 6, of which 5 were waited for; matrix products, arithmetic and copies ran while one was open for 8% of the time, Pallas kernels for 5%

profile of v2, /device:TPU:8, one launch (start us, length us, event | category | flops | bytes accessed | tf_op | source)
XLA Modules:
  0.0 116.4 jit_solution(413611116908618414)
XLA Ops:
  0.6 0.0 copy-start
  0.6 0.9 iota_compare_fusion.1
  1.5 0.7 reshape.137
  2.3 0.7 reshape.152
  3.0 0.7 reshape.148
  3.7 0.1 fusion.32
  3.8 0.0 copy-done
  3.8 0.7 fusion.31
  4.6 0.2 fusion.21
  4.9 0.4 copy-done.7
  5.3 0.4 fusion.15
  5.7 0.0 copy-start.4
  5.7 0.0 copy-start.3
  5.8 3.1 %convolution_convert_fusion = bf16[16,4608]{1,0:T(8,128)(2,1)S(1)} fusion(bf16[16,512]{1,0:T(8,128)(2,1)S(1)} %reshape.141, bf16[512,4608]{1,0:T(8,128)(2,1)} %param.19), kind=kOutput, calls=%fused_computation | convolution fusion | flops 75571200 | bytes 4882432 | tf_op jit(solution)/shard_map/dot_general | solution.py:237
  8.8 0.7 reshape.142
  9.6 8.5 %all-to-all-start = ((bf16[8,2,4608]{2,1,0:T(2,128)(2,1)}), bf16[8,2,4608]{2,1,0:T(2,128)(2,1)S(1)}, u32[]{:S(2)}, u32[]{:S(2)}) async-start(bf16[8,2,4608]{2,1,0:T(2,128)(2,1)} %reshape.142), calls=%async_computation | async-start | bytes 294912 | tf_op jit(solution)/shard_map/all_to_all | solution.py:56
  18.0 0.0 collective-permute-start.1
  18.1 9.4 %all-to-all-done = bf16[8,2,4608]{2,1,0:T(2,128)(2,1)S(1)} async-done(((bf16[8,2,4608]{2,1,0:T(2,128)(2,1)}), bf16[8,2,4608]{2,1,0:T(2,128)(2,1)S(1)}, u32[]{:S(2)}, u32[]{:S(2)}) %all-to-all-start) | async-done | bytes 147488 | tf_op jit(solution)/shard_map/all_to_all | solution.py:56
  27.5 0.1 convert_reduce_fusion
  27.6 0.2 multiply_reduce_fusion.1
  27.7 1.0 add_convert_fusion
  28.7 0.1 broadcast_in_dim.67
  28.8 11.6 %all_to_all.32 = bf16[8,2,4608]{2,1,0:T(2,128)(2,1)S(1)} all-to-all(bf16[8,2,4608]{2,1,0:T(2,128)(2,1)S(1)} %broadcast_in_dim.67), channel_id=1, replica_groups=mesh['dp_0'=4,'dp_1'=4,'dp_2'=2,'tensor'=8] {'tensor'}, dimensions={0} | all-to-all | bytes 294912 | tf_op jit(solution)/shard_map/all_to_all | solution.py:56
  40.5 0.2 multiply_reduce_fusion
  40.7 0.1 rsqrt.21
  40.8 0.1 reshape.143
  40.9 0.0 copy-start.6
  40.9 0.0 copy-start.5
  40.9 0.1 multiply_convert_fusion
  41.0 0.6 fusion.30
  41.7 1.1 broadcast_in_dim.70
  42.8 7.4 %all-to-all-start.3 = ((bf16[16,16,2304]{2,1,0:T(8,128)(2,1)}), bf16[16,16,2304]{2,1,0:T(8,128)(2,1)S(1)}, u32[]{:S(2)}, u32[]{:S(2)}) async-start(bf16[16,16,2304]{2,1,0:T(8,128)(2,1)} %broadcast_in_dim.70), calls=%async_computation.3 | async-start | bytes 2359296 | tf_op jit(solution)/shard_map/all_to_all | solution.py:56
  50.2 0.6 fusion.24
  51.5 0.1 collective-permute-start
  51.6 1.1 collective-permute-done
  52.7 0.5 slice.33
  53.9 0.1 copy.37
  54.0 0.9 fusion.19
  54.9 10.1 %all-to-all-done.3 = bf16[16,16,2304]{2,1,0:T(8,128)(2,1)S(1)} async-done(((bf16[16,16,2304]{2,1,0:T(8,128)(2,1)}), bf16[16,16,2304]{2,1,0:T(8,128)(2,1)S(1)}, u32[]{:S(2)}, u32[]{:S(2)}) %all-to-all-start.3) | async-done | bytes 1179680 | tf_op jit(solution)/shard_map/all_to_all | solution.py:56
  65.0 1.2 %broadcast_in_dim.69 = bf16[16,16,2432]{2,1,0:T(8,128)(2,1)} broadcast(bf16[16,2432]{1,0:T(8,128)(2,1)S(1)} %fusion.19), dimensions={1,2} | broadcast | bytes 1323008 | tf_op jit(solution)/shard_map/broadcast_in_dim | solution.py:63
  66.2 0.2 copy-done.2
  66.5 4.9 %all-to-all-start.2 = ((bf16[16,16,2432]{2,1,0:T(8,128)(2,1)}), bf16[16,16,2432]{2,1,0:T(8,128)(2,1)S(1)}, u32[]{:S(2)}, u32[]{:S(2)}) async-start(bf16[16,16,2432]{2,1,0:T(8,128)(2,1)} %broadcast_in_dim.69), calls=%async_computation.2 | async-start | bytes 2490368 | tf_op jit(solution)/shard_map/all_to_all | solution.py:56
  71.4 0.1 copy.32
  71.5 0.1 reduce.1
  71.6 0.6 pad_add_fusion.starts_ref
  72.2 0.7 constant_dynamic-slice_fusion
  72.9 6.3 %first_half.1.part_hbm = f32[4,256,256]{2,1,0:T(8,128)} custom-call(bf16[256,2304]{1,0:T(8,128)(2,1)} %bitcast.59, bf16[512,4608]{1,0:T(8,128)(2,1)} %own_hbm.3, bf16[512,4608]{1,0:T(8,128)(2,1)} %collective-permute-done.1.other_hbm), custom_call_target="tpu_custom_call" | custom-call | flops 1207959552 | bytes 4718592 | tf_op jit(solution)/shard_map/first_half/pallas_call | solution.py:117
  79.2 8.2 %all-to-all-done.2 = bf16[16,16,2432]{2,1,0:T(8,128)(2,1)S(1)} async-done(((bf16[16,16,2432]{2,1,0:T(8,128)(2,1)}), bf16[16,16,2432]{2,1,0:T(8,128)(2,1)S(1)}, u32[]{:S(2)}, u32[]{:S(2)}) %all-to-all-start.2) | async-done | bytes 1245216 | tf_op jit(solution)/shard_map/all_to_all | solution.py:56
  87.4 1.1 copy-done.1
  88.5 7.5 %second_half.1 = f32[8,256]{1,0:T(8,128)} custom-call(s32[2]{0:T(128)} %pad_add_fusion.starts_ref, bf16[256,2432]{1,0:T(8,128)(2,1)} %bitcast.58, bf16[512,4608]{1,0:T(8,128)(2,1)} %own_hbm.3, bf16[512,4608]{1,0:T(8,128)(2,1)} %collective-permute-done.1.other_hbm, f32[4,256,256]{2,1,0:T(8,128)} %first_half.1.part_hbm), custom_call_target="tpu_custom_call" | custom-call | flops 1207959552 | bytes 4718592 | tf_op jit(solution)/shard_map/second_half/pallas_call | solution.py:186
  96.0 0.8 slice_convert_fusion
  96.8 0.1 squeeze.11
  96.9 0.1 copy.36
  97.0 0.1 squeeze.10
  97.0 0.1 reduce_sum.97
  97.2 0.1 reshape.146
  97.3 0.1 broadcast_in_dim.71
  97.3 0.6 broadcast_in_dim.72
  98.0 6.6 %all-to-all-start.4 = ((f32[128,1,32]{2,1,0:T(1,128)}), f32[128,1,32]{2,1,0:T(1,128)S(1)}, u32[]{:S(2)}, u32[]{:S(2)}) async-start(f32[128,1,32]{2,1,0:T(1,128)} %bitcast.12), calls=%async_computation.4 | async-start | bytes 131072 | tf_op jit(solution)/shard_map/all_to_all | solution.py:56
  104.6 0.6 fusion.26
  105.9 0.5 compare_select_fusion.1
  106.4 9.3 %all-to-all-done.4 = f32[128,1,32]{2,1,0:T(1,128)S(1)} async-done(((f32[128,1,32]{2,1,0:T(1,128)}), f32[128,1,32]{2,1,0:T(1,128)S(1)}, u32[]{:S(2)}, u32[]{:S(2)}) %all-to-all-start.4) | async-done | bytes 16416 | tf_op jit(solution)/shard_map/all_to_all | solution.py:56
  115.8 0.1 exponential_reduce_fusion
  115.9 0.5 add_subtract_fusion
  (22 shorter events, 0.3 us)
Async XLA Ops:
  0.6 3.2 %copy-start = (bf16[16,256,256]{2,1,0:T(8,128)(2,1)S(1)}, bf16[16,256,256]{2,1,0:T(8,128)(2,1)}, u32[]{:S(2)}) copy-start(bf16[16,256,256]{2,1,0:T(8,128)(2,1)} %param.16) | copy-start | bytes 6291460
  3.7 1.6 %copy-start.7 = (bf16[16,256,256]{2,1,0:T(8,128)(2,1)S(1)}, bf16[16,256,256]{2,1,0:T(8,128)(2,1)}, u32[]{:S(2)}) copy-start(bf16[16,256,256]{2,1,0:T(8,128)(2,1)} %param.17) | copy-start | bytes 6291460
  5.7 22.0 %copy-start.4 = (f32[4608]{0:T(1024)S(1)}, f32[4608]{0:T(1024)}, u32[]{:S(2)}) copy-start(f32[4608]{0:T(1024)} %param.21) | copy-start | bytes 55300
  5.7 35.1 %copy-start.3 = (f32[4608]{0:T(1024)S(1)}, f32[4608]{0:T(1024)}, u32[]{:S(2)}) copy-start(f32[4608]{0:T(1024)} %param.22) | copy-start | bytes 55300
  9.6 17.9 %all-to-all-start = ((bf16[8,2,4608]{2,1,0:T(2,128)(2,1)}), bf16[8,2,4608]{2,1,0:T(2,128)(2,1)S(1)}, u32[]{:S(2)}, u32[]{:S(2)}) async-start(bf16[8,2,4608]{2,1,0:T(2,128)(2,1)} %reshape.142), calls=%async_computation | async-start | bytes 294912 | tf_op jit(solution)/shard_map/all_to_all | solution.py:56
  18.0 54.9 %collective-permute-start.1 = (bf16[512,4608]{1,0:T(8,128)(2,1)}, bf16[512,4608]{1,0:T(8,128)(2,1)}, u32[]{:S(2)}, u32[]{:S(2)}) collective-permute-start(bf16[512,4608]{1,0:T(8,128)(2,1)} %own_hbm.3), channel_id=1, source_target_pairs={{0,8},{8,0},{1,9},{9,1},{2,10},{10,2},{3,11},{11,3},{4,12},{12,4},... | collective-permute-start | bytes 14155784 | tf_op jit(solution)/shard_map/ppermute | solution.py:67
  40.9 9.3 %copy-start.6 = (s32[16]{0:T(128)S(1)}, s32[16]{0:T(128)}, u32[]{:S(2)}) copy-start(s32[16]{0:T(128)} %param.25) | copy-start | bytes 196
  40.9 10.7 %copy-start.5 = (s32[16]{0:T(128)S(1)}, s32[16]{0:T(128)}, u32[]{:S(2)}) copy-start(s32[16]{0:T(128)} %param.24) | copy-start | bytes 196
  42.8 22.2 %all-to-all-start.3 = ((bf16[16,16,2304]{2,1,0:T(8,128)(2,1)}), bf16[16,16,2304]{2,1,0:T(8,128)(2,1)S(1)}, u32[]{:S(2)}, u32[]{:S(2)}) async-start(bf16[16,16,2304]{2,1,0:T(8,128)(2,1)} %broadcast_in_dim.70), calls=%async_computation.3 | async-start | bytes 2359296 | tf_op jit(solution)/shard_map/all_to_all | solution.py:56
  51.5 1.3 %collective-permute-start = (f32[8,128]{1,0:T(8,128)S(1)}, f32[8,128]{1,0:T(8,128)S(1)}, u32[]{:S(2)}, u32[]{:S(2)}) collective-permute-start(f32[8,128]{1,0:T(8,128)S(1)} %broadcast_in_dim.68), channel_id=1, source_target_pairs={{0,8},{8,0},{1,9},{9,1},{2,10},{10,2},{3,11},{11,3},{4,12},{12,4},... | collective-permute-start | bytes 12296 | tf_op jit(solution)/shard_map/ppermute | solution.py:67
  65.0 1.4 %copy-start.2 = (bf16[16,16,2304]{2,1,0:T(8,128)(2,1)}, bf16[16,16,2304]{2,1,0:T(8,128)(2,1)S(1)}, u32[]{:S(2)}) copy-start(bf16[16,16,2304]{2,1,0:T(8,128)(2,1)S(1)} %all-to-all-done.3) | copy-start | bytes 3538948
  66.5 20.9 %all-to-all-start.2 = ((bf16[16,16,2432]{2,1,0:T(8,128)(2,1)}), bf16[16,16,2432]{2,1,0:T(8,128)(2,1)S(1)}, u32[]{:S(2)}, u32[]{:S(2)}) async-start(bf16[16,16,2432]{2,1,0:T(8,128)(2,1)} %broadcast_in_dim.69), calls=%async_computation.2 | async-start | bytes 2490368 | tf_op jit(solution)/shard_map/all_to_all | solution.py:56
  87.4 1.1 copy-start.1
  98.0 17.7 %all-to-all-start.4 = ((f32[128,1,32]{2,1,0:T(1,128)}), f32[128,1,32]{2,1,0:T(1,128)S(1)}, u32[]{:S(2)}, u32[]{:S(2)}) async-start(f32[128,1,32]{2,1,0:T(1,128)} %bitcast.12), calls=%async_computation.4 | async-start | bytes 131072 | tf_op jit(solution)/shard_map/all_to_all | solution.py:56

commit v3 on v1

v3 whole, which is shorter than its diff:
```python
import jax
import jax.numpy as jnp
from jax import lax
from jax.experimental import pallas as pl
from jax.experimental.pallas import tpu as pltpu
from jax.sharding import Mesh
from jax.sharding import PartitionSpec as P

D = 4608
HEADS = 32
KV_HEADS = 16
HEAD_DIM = 128
DP = ("dp_0", "dp_1", "dp_2")
DP_TENSOR = ("dp_0", "dp_1", "dp_2", "tensor")
PLANE = ("dp_0", "dp_1")
CHIPS = ("dp_0", "dp_1", "tensor")
META = 128


def attend_local(query, incoming_key, new_value, key_cache, value_cache, cache_len):
    slot_dev = query.shape[0]
    positions = key_cache.shape[1]
    kv_local = incoming_key.shape[1] // HEAD_DIM
    group = HEADS // KV_HEADS
    query_vector = query.reshape(slot_dev, kv_local, group, HEAD_DIM)
    keys = key_cache.reshape(slot_dev, positions, kv_local, HEAD_DIM)
    values = value_cache.reshape(slot_dev, positions, kv_local, HEAD_DIM)
    self_key = incoming_key.reshape(slot_dev, kv_local, HEAD_DIM)
    own_value = new_value.reshape(slot_dev, kv_local, HEAD_DIM).astype(jnp.float32)
    scores = (
        jnp.einsum("bkgd,bckd->bkgc", query_vector, keys, preferred_element_type=jnp.float32) / 12.0
    )
    self_entry = (
        jnp.einsum("qyxm,qym->qyx", query_vector, self_key, preferred_element_type=jnp.float32)
        / 12.0
    )
    valid = (
        jnp.arange(positions, dtype=jnp.int32)[None, None, None, :] < cache_len[:, None, None, None]
    )
    scores = jnp.where(valid, scores, -1e30)
    top = jnp.maximum(jnp.max(scores, axis=-1), self_entry)
    expo = jnp.where(valid, jnp.exp(scores - top[..., None]), 0.0)
    own_exp = jnp.exp(self_entry - top)
    total = jnp.sum(expo, axis=-1) + own_exp
    weight = (expo / total[..., None]).astype(jnp.bfloat16)
    own_weight = (own_exp / total).astype(jnp.bfloat16).astype(jnp.float32)
    attn = jnp.einsum("bkgc,bckd->bkgd", weight, values, preferred_element_type=jnp.float32)
    attn = attn + own_weight[..., None] * own_value[:, :, None, :]
    return attn.astype(jnp.bfloat16).reshape(slot_dev, kv_local * group * HEAD_DIM)


def exchange(blocks, axes):
    return lax.all_to_all(blocks, axes, 0, 0, tiled=True)


def other_core(value):
    return lax.ppermute(value, "dp_2", [(0, 1), (1, 0)])


def inverse_rms(rows):
    return lax.rsqrt(jnp.mean(rows * rows, axis=-1, keepdims=True) + 1e-06)


def product(rows, slots):
    return lax.dot_general(
        rows, slots, (((1,), (1,)), ((), ())), preferred_element_type=jnp.float32
    )


def in_vmem(count):
    return [pl.BlockSpec(memory_space=pltpu.VMEM)] * count


def params(mib):
    return pltpu.CompilerParams(vmem_limit_bytes=mib * 1024 * 1024)


def mix_kernel(pieces_ref, residual_ref, gain_ref, out_ref):
    nz, per, _ = pieces_ref.shape
    z = lax.axis_index("tensor")
    proj = pieces_ref[0].astype(jnp.float32)
    for k in range(1, nz):
        proj = proj + pieces_ref[k].astype(jnp.float32)
    post = proj * inverse_rms(proj) * gain_ref[...]
    residual = residual_ref[...].astype(jnp.float32)
    row = lax.broadcasted_iota(jnp.int32, (residual.shape[0], 1), 0)
    picked = [
        jnp.sum(jnp.where(row == z * per + k, residual, 0.0), axis=0, keepdims=True)
        for k in range(per)
    ]
    mix = (jnp.concatenate(picked, axis=0) + post).astype(jnp.bfloat16)
    for k in range(nz):
        out_ref[k] = mix


def mix_rows(pieces, residual, gain):
    return pl.pallas_call(
        mix_kernel,
        in_specs=in_vmem(3),
        out_specs=in_vmem(1)[0],
        out_shape=jax.ShapeDtypeStruct(pieces.shape, jnp.bfloat16),
        compiler_params=params(4),
        name="mix_rows",
    )(pieces, residual, gain)


def as_column(line):
    size = line.shape[1]
    row = lax.broadcasted_iota(jnp.int32, (size, size), 0)
    lane = lax.broadcasted_iota(jnp.int32, (size, size), 1)
    return jnp.sum(jnp.where(row == lane, line, 0), axis=1, keepdims=True)


def hidden_kernel(mix_ref, gain_ref, sampled_ref, flag_ref, other_ref, block_ref, slice_ref, rows):
    nz, per, _ = mix_ref.shape
    slot_dev, width = slice_ref.shape
    z = lax.axis_index("tensor")
    for k in range(nz):
        rows[k * per : (k + 1) * per, :] = mix_ref[k].astype(jnp.float32)
    mixed = rows[...]
    hidden = (mixed * inverse_rms(mixed) * gain_ref[...]).astype(jnp.bfloat16)
    sampled = sampled_ref[...]
    freed = (flag_ref[...] == 1).astype(jnp.int32)
    count = jnp.sum((other_ref[...] == 1).astype(jnp.int32), axis=1, keepdims=True)
    values = [sampled & 63, (sampled >> 6) & 63, sampled >> 12, freed]
    lane = lax.broadcasted_iota(jnp.int32, (slot_dev, META), 1)
    notes = jnp.where(lane == 4, count, 0)
    for k, value in enumerate(values):
        notes = jnp.where(lane == k, as_column(value), notes)
    notes = notes.astype(jnp.float32).astype(jnp.bfloat16)
    for k in range(block_ref.shape[0]):
        block_ref[k, :, :D] = hidden
        block_ref[k, :, D:] = notes
    for k in range(nz):

        @pl.when(z == k)
        def _():
            slice_ref[...] = rows[:, k * width : (k + 1) * width].astype(jnp.bfloat16)


def hidden_blocks(mix, gain, sampled, flag, other_flag, planes):
    slot_dev = mix.shape[0] * mix.shape[1]
    width = D // mix.shape[0]
    return pl.pallas_call(
        hidden_kernel,
        in_specs=in_vmem(5),
        out_specs=in_vmem(2),
        out_shape=[
            jax.ShapeDtypeStruct((planes, slot_dev, D + META), jnp.bfloat16),
            jax.ShapeDtypeStruct((slot_dev, width), jnp.bfloat16),
        ],
        scratch_shapes=[pltpu.VMEM((slot_dev, D), jnp.float32)],
        compiler_params=params(8),
        name="hidden_blocks",
    )(mix, gain, sampled, flag, other_flag)


def vocab_kernel(every_ref, own_ref, other_ref, flag_ref, pair_ref, rank_ref, total_ref):
    slots = every_ref.shape[0]
    per_device = own_ref.shape[0]
    slot_dev = flag_ref.shape[1]
    planes = slots // slot_dev
    nz = pair_ref.shape[0] // planes
    z = lax.axis_index("tensor")
    core = lax.axis_index("dp_2")
    plane = lax.axis_index("dp_0") * lax.axis_size("dp_1") + lax.axis_index("dp_1")
    every = every_ref[:, :D]
    lane = lax.broadcasted_iota(jnp.int32, (16, META), 1)
    row = lax.broadcasted_iota(jnp.int32, (16, META), 0)
    digit = jnp.where(lane == 0, 1.0, jnp.where(lane == 1, 64.0, jnp.where(lane == 2, 4096.0, 0.0)))
    pick = jnp.where(row == 0, digit, jnp.where(lane == row + 2, 1.0, 0.0))
    notes = product(pick.astype(jnp.bfloat16), every_ref[:, D:])
    ids = notes[0:1, :].astype(jnp.int32)
    line = lax.broadcasted_iota(jnp.int32, (per_device, slots), 0)
    tops, sums = [], []
    picked = jnp.zeros((1, slots), jnp.float32)
    for weight_ref, holder in ((own_ref, core), (other_ref, 1 - core)):
        begin = ((plane * 2 + holder) * nz + z) * per_device
        logits = product(weight_ref[...], every)
        picked = picked + jnp.sum(jnp.where(line == ids - begin, logits, 0.0), axis=0, keepdims=True)
        top = jnp.max(logits, axis=0, keepdims=True)
        tops.append(top)
        sums.append(jnp.sum(jnp.exp(logits - top), axis=0, keepdims=True))
    top = jnp.maximum(tops[0], tops[1])
    total = sums[0] * jnp.exp(tops[0] - top) + sums[1] * jnp.exp(tops[1] - top)
    entropy = top + jnp.log(total)
    for k in range(planes):
        for part, value in ((0, entropy), (1, picked)):
            pair_ref[k * nz : (k + 1) * nz, part * slot_dev : (part + 1) * slot_dev] = (
                jnp.broadcast_to(value[:, k * slot_dev : (k + 1) * slot_dev], (nz, slot_dev))
            )

    slot = lax.broadcasted_iota(jnp.int32, (1, slots), 1)
    flags = notes[1:2, :]
    counts = jnp.where(slot % slot_dev == 0, notes[2:3, :], 0.0)
    both = flags + counts
    total_ref[...] = jnp.sum(both, axis=1, keepdims=True).astype(jnp.int32)
    before = jnp.sum(jnp.where(slot // slot_dev < plane, both, 0.0), axis=1, keepdims=True)
    partner = jnp.sum(jnp.where(slot == plane * slot_dev, counts, 0.0), axis=1, keepdims=True)
    before = (before + jnp.where(core == 1, partner, 0.0)).astype(jnp.int32)
    freed = (flag_ref[...] == 1).astype(jnp.int32)
    below = lax.broadcasted_iota(jnp.int32, (slot_dev, slot_dev), 0)
    place = lax.broadcasted_iota(jnp.int32, (slot_dev, slot_dev), 1)
    ahead = jnp.sum(jnp.where(below < place, as_column(freed), 0), axis=0, keepdims=True)
    rank_ref[...] = jnp.where(freed == 1, ahead + before, -1)


def vocab_stats(every, own, other, flag, nz):
    slots = every.shape[0]
    rows = own.shape[0]
    slot_dev = flag.shape[1]
    return pl.pallas_call(
        vocab_kernel,
        in_specs=in_vmem(4),
        out_specs=in_vmem(3),
        out_shape=[
            jax.ShapeDtypeStruct((slots // slot_dev * nz, 2 * slot_dev), jnp.float32),
            jax.ShapeDtypeStruct((1, slot_dev), jnp.int32),
            jax.ShapeDtypeStruct((1, 1), jnp.int32),
        ],
        compiler_params=params(24),
        cost_estimate=pl.CostEstimate(
            flops=4 * rows * slots * D, bytes_accessed=4 * rows * D, transcendentals=2 * rows * slots
        ),
        name="vocab_stats",
    )(every, own, other, flag)


def on_device(
    query,
    incoming_key,
    new_value,
    key_cache,
    value_cache,
    cache_len,
    out_weight,
    residual,
    post_gain,
    final_gain,
    vocab_weight,
    sampled,
    stop_flag,
):
    slot_dev = query.shape[0]
    nz = lax.axis_size("tensor")
    planes = lax.axis_size(PLANE)
    vocab_other = other_core(vocab_weight)
    other_flag = other_core(stop_flag)

    attn = attend_local(query, incoming_key, new_value, key_cache, value_cache, cache_len)
    partial_value = jnp.dot(attn, out_weight, preferred_element_type=jnp.float32)
    blocks = partial_value.astype(jnp.bfloat16).reshape(nz, slot_dev // nz, D)
    post_line, final_line = post_gain.reshape(1, D), final_gain.reshape(1, D)
    flag, sampled_line = stop_flag.reshape(1, slot_dev), sampled.reshape(1, slot_dev)
    blocks, vocab_other, other_flag, post_line, final_line, flag, sampled_line = (
        lax.optimization_barrier(
            (blocks, vocab_other, other_flag, post_line, final_line, flag, sampled_line)
        )
    )
    pieces = exchange(blocks, "tensor")
    mix = exchange(mix_rows(pieces, residual, post_line), "tensor")
    hidden, new_residual = hidden_blocks(
        mix,
        final_line,
        sampled_line,
        flag,
        other_flag.reshape(1, slot_dev),
        planes,
    )
    every = exchange(hidden, PLANE).reshape(planes * slot_dev, D + META)
    pair, rank, released = vocab_stats(every, vocab_weight, vocab_other, flag, nz)
    gathered = exchange(pair, CHIPS)
    parts = gathered[:, :slot_dev]
    highest = jnp.max(parts, axis=0)
    overall = jnp.log(jnp.sum(jnp.exp(parts - highest[None]), axis=0)) + highest
    token_logprob = jnp.sum(gathered[:, slot_dev:], axis=0) - overall
    return (new_residual, token_logprob, rank.reshape(slot_dev), released.reshape(()))


def solution(mesh):
    split = Mesh(
        mesh.devices.reshape(4, 4, 2, mesh.shape["tensor"]), ("dp_0", "dp_1", "dp_2", "tensor")
    )
    in_specs = (
        P(DP, "tensor"),
        P(DP, "tensor"),
        P(DP, "tensor"),
        P(DP, None, "tensor"),
        P(DP, None, "tensor"),
        P(DP),
        P("tensor", None),
        P(DP, None),
        P(),
        P(),
        P(DP_TENSOR, None),
        P(DP),
        P(DP),
    )
    out_specs = (P(DP, "tensor"), P(DP), P(DP), P())
    return jax.shard_map(
        on_device, mesh=split, in_specs=in_specs, out_specs=out_specs, check_vma=False
    )
```

time: 115 us -> 103 us (0.90)
  blocking collectives: 0 us -> 81.9 us
  waiting for transfers between devices: 54.7 us -> 0.01 us
  starting transfers between devices: 27.2 us -> 0.59 us
  matrix products: 15.1 us -> 4.45 us
  Pallas kernels: 0 us -> 6.5 us
  other arithmetic: 7.32 us -> 1.67 us
  between operations: 2.88 us -> 0.77 us
  local copies, waits for them, and re-layouts: 7.65 us -> 6.27 us
    all_to_all x0 -> x4, blocking collectives: none -> 81.9 us  [exchange(): return lax.all_to_all(blocks, axes, 0, 0, tiled=True)]
    all_to_all x4 -> x0, waiting for transfers between devices: 54.7 us -> none  [exchange(): return lax.all_to_all(blocks, axes, 0, 0, tiled=True)]
    all_to_all x4 -> x0, starting transfers between devices: 26.6 us -> none  [exchange(): return lax.all_to_all(blocks, axes, 0, 0, tiled=True)]
    dot_general x2 -> x0, matrix products: 9.09 us -> none  [vocab_part(): lax.dot_general(every, rows, (((1,), (1,)), ((), ())), preferred_element_...]
    pallas_call x0 -> x3, Pallas kernels: none -> 6.5 us  [the longest x1 5.29 us: vocab_stats(): pl.pallas_call(vocab_kernel, in_specs=in_vmem(4), out_specs=in_vmem(3), o...]
    broadcast_in_dim x5 -> x0, local copies, waits for them, and re-layouts: 3.1 us -> none  [the longest x2 2.39 us: spread(): return exchange(jnp.broadcast_to(block[None], (count, *block.shape)), axes)]
    reduce_sum x7 -> x0, other arithmetic: 2.41 us -> none  [the longest x1 0.65 us: on_device(): released = jnp.sum(both).astype(jnp.int32)]
    unnamed x13 -> x12, local copies, waits for them, and re-layouts: 0.14 us -> 2.37 us
  transfers between devices with their start and end apart: 6 -> 2, of which waited for: 4 -> 0; matrix products, arithmetic and copies ran while one was open for 12% -> 9% of each run, Pallas kernels for 0% -> 0%
where the time goes in v3:
time: 103 us; the launch traced here: 102 us
  blocking collectives  81.9 us (80%)
  Pallas kernels  6.5 us (6%)
  local copies, waits for them, and re-layouts  6.27 us (6%)
  matrix products  4.45 us (4%)
  other arithmetic  1.67 us (2%)
    all_to_all x4, blocking collectives, exchange(): return lax.all_to_all(blocks, axes, 0, 0, tiled=True)  81.9 us
    pallas_call x1, Pallas kernels, vocab_stats(): pl.pallas_call(vocab_kernel, in_specs=in_vmem(4), out_specs=in_vmem(3), o...  5.29 us
    dot_general x1, matrix products, on_device(): jnp.dot(attn, out_weight, preferred_element_type=jnp.float32)  3.13 us
    unnamed x12, local copies, waits for them, and re-layouts  2.37 us
  transfers between devices with their start and end apart: 2, of which 0 were waited for; matrix products, arithmetic and copies ran while one was open for 9% of the time, Pallas kernels for 0%

profile of v3, /device:TPU:8, one launch (start us, length us, event | category | flops | bytes accessed | tf_op | source)
XLA Modules:
  0.0 102.1 jit_solution(17785673696145662765)
XLA Ops:
  0.6 0.0 copy-start
  0.6 0.1 collective-permute-start
  0.7 0.5 collective-permute-start.1
  1.2 0.8 reshape.85
  2.0 0.7 reshape.103
  2.7 0.7 reshape.99
  3.4 0.0 copy-start.5
  3.4 0.9 reshape.91.gain_ref
  4.3 0.7 reshape.92.gain_ref
  5.1 0.7 iota_compare_fusion
  5.8 0.1 fusion.24
  6.0 0.0 copy-done
  6.0 0.7 fusion.23
  6.7 0.2 fusion.19
  7.0 0.0 copy-done.5
  7.0 0.4 fusion.15
  7.5 0.0 copy-start.2
  7.5 0.0 copy-start.3
  7.5 0.0 copy-start.4
  7.5 3.1 %convolution_convert_fusion = bf16[16,4608]{1,0:T(8,128)(2,1)S(1)} fusion(bf16[16,512]{1,0:T(8,128)(2,1)S(1)} %reshape.89, bf16[512,4608]{1,0:T(8,128)(2,1)} %param.19), kind=kOutput, calls=%fused_computation | convolution fusion | flops 75571200 | bytes 4882432 | tf_op jit(solution)/shard_map/dot_general | solution.py:251
  10.6 0.1 reshape.90
  10.7 0.0 collective-permute-done.1
  10.7 0.0 collective-permute-done.other_ref
  10.7 17.9 %all_to_all.27.pieces_ref = bf16[8,2,4608]{2,1,0:T(2,128)(2,1)S(1)} all-to-all(bf16[8,2,4608]{2,1,0:T(2,128)(2,1)S(1)} %reshape.90), channel_id=1, replica_groups=mesh['dp_0'=4,'dp_1'=4,'dp_2'=2,'tensor'=8] {'tensor'}, dimensions={0} | all-to-all | bytes 294912 | tf_op jit(solution)/shard_map/all_to_all | solution.py:53
  28.6 0.0 copy-done.2
  28.7 0.2 mix_rows.1
  28.9 11.6 %all_to_all.28.mix_ref = bf16[8,2,4608]{2,1,0:T(2,128)(2,1)S(1)} all-to-all(bf16[8,2,4608]{2,1,0:T(2,128)(2,1)S(1)} %mix_rows.1), channel_id=1, replica_groups=mesh['dp_0'=4,'dp_1'=4,'dp_2'=2,'tensor'=8] {'tensor'}, dimensions={0} | all-to-all | bytes 294912 | tf_op jit(solution)/shard_map/all_to_all | solution.py:53
  40.5 0.0 copy-done.3
  40.5 0.0 copy-done.4
  40.5 1.0 hidden_blocks.1
  41.5 34.7 %all_to_all.29 = bf16[16,16,4736]{2,1,0:T(8,128)(2,1)S(1)} all-to-all(bf16[16,16,4736]{2,1,0:T(8,128)(2,1)S(1)} %get-tuple-element.23), channel_id=1, replica_groups=mesh['dp_0'=4,'dp_1'=4,'dp_2'=2,'tensor'=8] {'dp_0','dp_1'}, dimensions={0} | all-to-all | bytes 4849664 | tf_op jit(solution)/shard_map/all_to_all | solution.py:53
  76.2 0.0 copy-start.1
  76.2 2.3 %copy-done.1 = bf16[512,4608]{1,0:T(8,128)(2,1)S(1)} copy-done((bf16[512,4608]{1,0:T(8,128)(2,1)S(1)}, bf16[512,4608]{1,0:T(8,128)(2,1)}, u32[]{:S(2)}) %copy-start.1) | copy-done | bytes 4718616
  78.5 5.3 %vocab_stats.1 = (f32[128,32]{1,0:T(8,128)S(1)}, s32[1,16]{1,0:T(1,128)}, s32[1,1]{1,0:T(1,128)}) custom-call(bf16[256,4736]{1,0:T(8,128)(2,1)S(1)} %bitcast.41, bf16[512,4608]{1,0:T(8,128)(2,1)S(1)} %copy-done.1, bf16[512,4608]{1,0:T(8,128)(2,1)} %collective-permute-done.other_ref, s32[1,16]{1,0:T(1,128)S(1)} %bitcast.44), custom_call_target="tpu_custom_call" | custom-call | flops 2415919104 | bytes 9437184 | tf_op jit(solution)/shard_map/vocab_stats/pallas_call | solution.py:212
  83.8 17.6 %all_to_all.30 = f32[128,1,32]{2,1,0:T(1,128)S(1)} all-to-all(f32[128,1,32]{2,1,0:T(1,128)S(1)} %bitcast.42), channel_id=1, replica_groups=mesh['dp_0'=4,'dp_1'=4,'dp_2'=2,'tensor'=8] {'dp_0','dp_1','tensor'}, dimensions={0} | all-to-all | bytes 32768 | tf_op jit(solution)/shard_map/all_to_all | solution.py:53
  101.5 0.1 exponential_reduce_fusion
  101.6 0.5 add_subtract_fusion
  (4 shorter events, 0.1 us)
Async XLA Ops:
  0.6 5.3 %copy-start = (bf16[16,256,256]{2,1,0:T(8,128)(2,1)S(1)}, bf16[16,256,256]{2,1,0:T(8,128)(2,1)}, u32[]{:S(2)}) copy-start(bf16[16,256,256]{2,1,0:T(8,128)(2,1)} %param.16) | copy-start | bytes 6291460
  0.6 10.1 %collective-permute-start = (bf16[512,4608]{1,0:T(8,128)(2,1)}, bf16[512,4608]{1,0:T(8,128)(2,1)}, u32[]{:S(2)}, u32[]{:S(2)}) collective-permute-start(bf16[512,4608]{1,0:T(8,128)(2,1)} %own_ref.1), channel_id=1, source_target_pairs={{0,8},{8,0},{1,9},{9,1},{2,10},{10,2},{3,11},{11,3},{4,12},{12,4},... | collective-permute-start | bytes 14155784 | tf_op jit(solution)/shard_map/ppermute | solution.py:57
  0.7 10.0 %collective-permute-start.1 = (s32[16]{0:T(128)}, s32[16]{0:T(128)S(1)}, u32[]{:S(2)}, u32[]{:S(2)}) collective-permute-start(s32[16]{0:T(128)} %param.25), channel_id=1, source_target_pairs={{0,8},{8,0},{1,9},{9,1},{2,10},{10,2},{3,11},{11,3},{4,12},{12,4},... | collective-permute-start | bytes 200 | tf_op jit(solution)/shard_map/ppermute | solution.py:57
  3.4 3.6 %copy-start.5 = (bf16[16,256,256]{2,1,0:T(8,128)(2,1)S(1)}, bf16[16,256,256]{2,1,0:T(8,128)(2,1)}, u32[]{:S(2)}) copy-start(bf16[16,256,256]{2,1,0:T(8,128)(2,1)} %param.17) | copy-start | bytes 6291460
  7.5 21.2 %copy-start.2 = (bf16[16,4608]{1,0:T(8,128)(2,1)S(1)}, bf16[16,4608]{1,0:T(8,128)(2,1)}, u32[]{:S(2)}) copy-start(bf16[16,4608]{1,0:T(8,128)(2,1)} %residual_ref.1) | copy-start | bytes 442372
  7.5 33.0 %copy-start.3 = (s32[16]{0:T(128)S(1)}, s32[16]{0:T(128)}, u32[]{:S(2)}) copy-start(s32[16]{0:T(128)} %param.25) | copy-start | bytes 196
  7.5 33.0 %copy-start.4 = (s32[16]{0:T(128)S(1)}, s32[16]{0:T(128)}, u32[]{:S(2)}) copy-start(s32[16]{0:T(128)} %param.24) | copy-start | bytes 196
  76.2 2.3 %copy-start.1 = (bf16[512,4608]{1,0:T(8,128)(2,1)S(1)}, bf16[512,4608]{1,0:T(8,128)(2,1)}, u32[]{:S(2)}) copy-start(bf16[512,4608]{1,0:T(8,128)(2,1)} %own_ref.1) | copy-start | bytes 14155780

commit v4 on v3

--- a/solution.py
+++ b/solution.py
@@ -15,38 +15,139 @@
 PLANE = ("dp_0", "dp_1")
 CHIPS = ("dp_0", "dp_1", "tensor")
 META = 128
-
-
-def attend_local(query, incoming_key, new_value, key_cache, value_cache, cache_len):
+CHUNKS = 4
+
+
+def attend_kernel(
+    len_ref, query_hbm, key_hbm, value_hbm, keys_hbm, values_hbm, weight_hbm, out_hbm,
+    keys, values, weight, query_ref, key_ref, value_ref, out_ref,
+    query_s, key_s, value_s, score_s, attn_s, part_s, key_sem, value_sem, weight_sem, small_sem,
+):
+    slot_dev = keys.shape[0]
+    positions = keys.shape[1]
+    group = HEADS // KV_HEADS
+    heads = query_ref.shape[1] // HEAD_DIM
+    kv_local = heads // group
+    batch = slot_dev // key_sem.shape[0]
+    chunk = D // weight_sem.shape[0]
+    loads = {}
+    smalls = ((query_hbm, query_ref), (key_hbm, key_ref), (value_hbm, value_ref))
+    for k, (source, target) in enumerate(smalls):
+        loads["s", k] = pltpu.make_async_copy(source, target, small_sem.at[k])
+        loads["s", k].start()
+    for name, source, target, sem in (("k", keys_hbm, keys, key_sem), ("v", values_hbm, values, value_sem)):
+        for k in range(sem.shape[0]):
+            part = pl.ds(k * batch, batch)
+            loads[name, k] = pltpu.make_async_copy(source.at[part], target.at[part], sem.at[k])
+            loads[name, k].start()
+    for k in range(weight_sem.shape[0]):
+        part = pl.ds(k * chunk, chunk)
+        loads["w", k] = pltpu.make_async_copy(
+            weight_hbm.at[:, part], weight.at[:, part], weight_sem.at[k]
+        )
+        loads["w", k].start()
+
+    for k in range(len(smalls)):
+        loads["s", k].wait()
+    for h in range(heads):
+        at = pl.ds(h, slot_dev, stride=heads)
+        kv = h // group * HEAD_DIM
+        query_s[at, :] = query_ref[:, h * HEAD_DIM : (h + 1) * HEAD_DIM].astype(jnp.float32)
+        key_s[at, :] = key_ref[:, kv : kv + HEAD_DIM].astype(jnp.float32)
+        value_s[at, :] = value_ref[:, kv : kv + HEAD_DIM].astype(jnp.float32)
+
+    lines = 8
+    pair = lines // heads
+    row = lax.broadcasted_iota(jnp.int32, (lines, 1), 0)
+    kind = row % heads // group
+
+    def per_slot(rows, source, first, contract):
+        found = None
+        for k in range(pair):
+            part = lax.dot_general(
+                rows, source[first + k], (((1,), (contract,)), ((), ())), preferred_element_type=jnp.float32
+            )
+            found = part if found is None else jnp.where(row >= k * heads, part, found)
+        return found
+
+    for i in range(slot_dev // pair):
+        if i * pair % batch == 0:
+            loads["k", i * pair // batch].wait()
+        rows = query_s[i * lines : (i + 1) * lines, :]
+        spread = [jnp.where(kind == k, rows, 0.0) for k in range(kv_local)]
+        spread = jnp.concatenate(spread, axis=1).astype(jnp.bfloat16)
+        score_s[i * lines : (i + 1) * lines, :] = per_slot(spread, keys, i * pair, 1)
+
+    total_rows = slot_dev * heads
+    owner = lax.broadcasted_iota(jnp.int32, (total_rows, 1), 0) // heads
+    length = jnp.zeros((total_rows, 1), jnp.int32)
+    for k in range(slot_dev):
+        length = jnp.where(owner == k, len_ref[k], length)
+    valid = lax.broadcasted_iota(jnp.int32, (total_rows, positions), 1) < length
+    scores = jnp.where(valid, score_s[...] / 12.0, -1e30)
+    own = jnp.sum(query_s[...] * key_s[...], axis=1, keepdims=True) / 12.0
+    top = jnp.maximum(jnp.max(scores, axis=1, keepdims=True), own)
+    expo = jnp.where(valid, jnp.exp(scores - top), 0.0)
+    own_exp = jnp.exp(own - top)
+    total = jnp.sum(expo, axis=1, keepdims=True) + own_exp
+    score_s[...] = expo / total
+    own_weight = (own_exp / total).astype(jnp.bfloat16).astype(jnp.float32)
+
+    for i in range(slot_dev // pair):
+        if i * pair % batch == 0:
+            loads["v", i * pair // batch].wait()
+        rows = score_s[i * lines : (i + 1) * lines, :].astype(jnp.bfloat16)
+        mixed = per_slot(rows, values, i * pair, 0)
+        found = mixed[:, :HEAD_DIM]
+        for k in range(1, kv_local):
+            found = jnp.where(kind == k, mixed[:, k * HEAD_DIM : (k + 1) * HEAD_DIM], found)
+        attn_s[i * lines : (i + 1) * lines, :] = found
+    attn_s[...] += own_weight * value_s[...]
+    attn = [attn_s[pl.ds(h, slot_dev, stride=heads), :] for h in range(heads)]
+    attn = jnp.concatenate(attn, axis=1).astype(jnp.bfloat16)
+    for k in range(weight_sem.shape[0]):
+        loads["w", k].wait()
+        part_s[:, k * chunk : (k + 1) * chunk] = jnp.dot(
+            attn, weight[:, k * chunk : (k + 1) * chunk], preferred_element_type=jnp.float32
+        )
+    per = out_ref.shape[1]
+    for k in range(out_ref.shape[0]):
+        out_ref[k] = part_s[k * per : (k + 1) * per, :].astype(jnp.bfloat16)
+    store = pltpu.make_async_copy(out_ref, out_hbm, small_sem.at[0])
+    store.start()
+    store.wait()
+
+
+def attend(query, incoming_key, new_value, key_cache, value_cache, cache_len, out_weight, nz):
     slot_dev = query.shape[0]
-    positions = key_cache.shape[1]
-    kv_local = incoming_key.shape[1] // HEAD_DIM
-    group = HEADS // KV_HEADS
-    query_vector = query.reshape(slot_dev, kv_local, group, HEAD_DIM)
-    keys = key_cache.reshape(slot_dev, positions, kv_local, HEAD_DIM)
-    values = value_cache.reshape(slot_dev, positions, kv_local, HEAD_DIM)
-    self_key = incoming_key.reshape(slot_dev, kv_local, HEAD_DIM)
-    own_value = new_value.reshape(slot_dev, kv_local, HEAD_DIM).astype(jnp.float32)
-    scores = (
-        jnp.einsum("bkgd,bckd->bkgc", query_vector, keys, preferred_element_type=jnp.float32) / 12.0
-    )
-    self_entry = (
-        jnp.einsum("qyxm,qym->qyx", query_vector, self_key, preferred_element_type=jnp.float32)
-        / 12.0
-    )
-    valid = (
-        jnp.arange(positions, dtype=jnp.int32)[None, None, None, :] < cache_len[:, None, None, None]
-    )
-    scores = jnp.where(valid, scores, -1e30)
-    top = jnp.maximum(jnp.max(scores, axis=-1), self_entry)
-    expo = jnp.where(valid, jnp.exp(scores - top[..., None]), 0.0)
-    own_exp = jnp.exp(self_entry - top)
-    total = jnp.sum(expo, axis=-1) + own_exp
-    weight = (expo / total[..., None]).astype(jnp.bfloat16)
-    own_weight = (own_exp / total).astype(jnp.bfloat16).astype(jnp.float32)
-    attn = jnp.einsum("bkgc,bckd->bkgd", weight, values, preferred_element_type=jnp.float32)
-    attn = attn + own_weight[..., None] * own_value[:, :, None, :]
-    return attn.astype(jnp.bfloat16).reshape(slot_dev, kv_local * group * HEAD_DIM)
+    lines = slot_dev * (query.shape[1] // HEAD_DIM)
+    hbm = pl.BlockSpec(memory_space=pltpu.HBM)
+    return pl.pallas_call(
+        attend_kernel,
+        in_specs=[pl.BlockSpec(memory_space=pltpu.SMEM), *[hbm] * 6],
+        out_specs=hbm,
+        out_shape=jax.ShapeDtypeStruct((nz, slot_dev // nz, D), jnp.bfloat16),
+        scratch_shapes=[
+            pltpu.VMEM(key_cache.shape, jnp.bfloat16),
+            pltpu.VMEM(value_cache.shape, jnp.bfloat16),
+            pltpu.VMEM(out_weight.shape, jnp.bfloat16),
+            pltpu.VMEM(query.shape, jnp.bfloat16),
+            pltpu.VMEM(incoming_key.shape, jnp.bfloat16),
+            pltpu.VMEM(new_value.shape, jnp.bfloat16),
+            pltpu.VMEM((nz, slot_dev // nz, D), jnp.bfloat16),
+            *[pltpu.VMEM((lines, HEAD_DIM), jnp.float32)] * 3,
+            pltpu.VMEM((lines, key_cache.shape[1]), jnp.float32),
+            pltpu.VMEM((lines, HEAD_DIM), jnp.float32),
+            pltpu.VMEM((slot_dev, D), jnp.float32),
+            pltpu.SemaphoreType.DMA((4,)),
+            pltpu.SemaphoreType.DMA((4,)),
+            pltpu.SemaphoreType.DMA((4,)),
+            pltpu.SemaphoreType.DMA((3,)),
+        ],
+        compiler_params=params(61),
+        cost_estimate=pl.CostEstimate(flops=2_000_000_000, bytes_accessed=9_000_000, transcendentals=20_000),
+        name="attend",
+    )(cache_len, query, incoming_key, new_value, key_cache, value_cache, out_weight)
 
 
 def exchange(blocks, axes):
@@ -81,7 +182,7 @@
     proj = pieces_ref[0].astype(jnp.float32)
     for k in range(1, nz):
         proj = proj + pieces_ref[k].astype(jnp.float32)
-    post = proj * inverse_rms(proj) * gain_ref[...]
+    post = proj * inverse_rms(proj) * gain_ref[...].reshape(1, D)
     residual = residual_ref[...].astype(jnp.float32)
     row = lax.broadcasted_iota(jnp.int32, (residual.shape[0], 1), 0)
     picked = [
@@ -118,7 +219,7 @@
     for k in range(nz):
         rows[k * per : (k + 1) * per, :] = mix_ref[k].astype(jnp.float32)
     mixed = rows[...]
-    hidden = (mixed * inverse_rms(mixed) * gain_ref[...]).astype(jnp.bfloat16)
+    hidden = (mixed * inverse_rms(mixed) * gain_ref[...].reshape(1, D)).astype(jnp.bfloat16)
     sampled = sampled_ref[...]
     freed = (flag_ref[...] == 1).astype(jnp.int32)
     count = jnp.sum((other_ref[...] == 1).astype(jnp.int32), axis=1, keepdims=True)
@@ -155,28 +256,45 @@
     )(mix, gain, sampled, flag, other_flag)
 
 
-def vocab_kernel(every_ref, own_ref, other_ref, flag_ref, pair_ref, rank_ref, total_ref):
+def vocab_kernel(
+    every_ref, own_hbm, other_hbm, flag_ref, pair_ref, rank_ref, total_ref, weights, logits_s, sems
+):
     slots = every_ref.shape[0]
-    per_device = own_ref.shape[0]
+    per_device = own_hbm.shape[0]
+    chunk = weights.shape[2]
+    loads = []
+    for k in range(weights.shape[0]):
+        for which, source in enumerate((own_hbm, other_hbm)):
+            copy = pltpu.make_async_copy(
+                source.at[:, pl.ds(k * chunk, chunk)],
+                weights.at[k, pl.ds(which * per_device, per_device)],
+                sems.at[k, which],
+            )
+            copy.start()
+            loads.append(copy)
     slot_dev = flag_ref.shape[1]
     planes = slots // slot_dev
     nz = pair_ref.shape[0] // planes
     z = lax.axis_index("tensor")
     core = lax.axis_index("dp_2")
     plane = lax.axis_index("dp_0") * lax.axis_size("dp_1") + lax.axis_index("dp_1")
-    every = every_ref[:, :D]
     lane = lax.broadcasted_iota(jnp.int32, (16, META), 1)
     row = lax.broadcasted_iota(jnp.int32, (16, META), 0)
     digit = jnp.where(lane == 0, 1.0, jnp.where(lane == 1, 64.0, jnp.where(lane == 2, 4096.0, 0.0)))
     pick = jnp.where(row == 0, digit, jnp.where(lane == row + 2, 1.0, 0.0))
     notes = product(pick.astype(jnp.bfloat16), every_ref[:, D:])
     ids = notes[0:1, :].astype(jnp.int32)
+    for k in range(weights.shape[0]):
+        loads[2 * k].wait()
+        loads[2 * k + 1].wait()
+        part = product(weights[k], every_ref[:, k * chunk : (k + 1) * chunk])
+        logits_s[...] = part if k == 0 else logits_s[...] + part
     line = lax.broadcasted_iota(jnp.int32, (per_device, slots), 0)
     tops, sums = [], []
     picked = jnp.zeros((1, slots), jnp.float32)
-    for weight_ref, holder in ((own_ref, core), (other_ref, 1 - core)):
+    for which, holder in enumerate((core, 1 - core)):
         begin = ((plane * 2 + holder) * nz + z) * per_device
-        logits = product(weight_ref[...], every)
+        logits = logits_s[which * per_device : (which + 1) * per_device, :]
         picked = picked + jnp.sum(jnp.where(line == ids - begin, logits, 0.0), axis=0, keepdims=True)
         top = jnp.max(logits, axis=0, keepdims=True)
         tops.append(top)
@@ -209,16 +327,22 @@
     slots = every.shape[0]
     rows = own.shape[0]
     slot_dev = flag.shape[1]
+    hbm = pl.BlockSpec(memory_space=pltpu.HBM)
     return pl.pallas_call(
         vocab_kernel,
-        in_specs=in_vmem(4),
+        in_specs=[*in_vmem(1), hbm, hbm, *in_vmem(1)],
         out_specs=in_vmem(3),
         out_shape=[
             jax.ShapeDtypeStruct((slots // slot_dev * nz, 2 * slot_dev), jnp.float32),
             jax.ShapeDtypeStruct((1, slot_dev), jnp.int32),
             jax.ShapeDtypeStruct((1, 1), jnp.int32),
         ],
-        compiler_params=params(24),
+        scratch_shapes=[
+            pltpu.VMEM((CHUNKS, 2 * rows, D // CHUNKS), jnp.bfloat16),
+            pltpu.VMEM((2 * rows, slots), jnp.float32),
+            pltpu.SemaphoreType.DMA((CHUNKS, 2)),
+        ],
+        compiler_params=params(50),
         cost_estimate=pl.CostEstimate(
             flops=4 * rows * slots * D, bytes_accessed=4 * rows * D, transcendentals=2 * rows * slots
         ),
@@ -247,21 +371,18 @@
     vocab_other = other_core(vocab_weight)
     other_flag = other_core(stop_flag)
 
-    attn = attend_local(query, incoming_key, new_value, key_cache, value_cache, cache_len)
-    partial_value = jnp.dot(attn, out_weight, preferred_element_type=jnp.float32)
-    blocks = partial_value.astype(jnp.bfloat16).reshape(nz, slot_dev // nz, D)
-    post_line, final_line = post_gain.reshape(1, D), final_gain.reshape(1, D)
+    blocks = attend(
+        query, incoming_key, new_value, key_cache, value_cache, cache_len, out_weight, nz
+    )
     flag, sampled_line = stop_flag.reshape(1, slot_dev), sampled.reshape(1, slot_dev)
-    blocks, vocab_other, other_flag, post_line, final_line, flag, sampled_line = (
-        lax.optimization_barrier(
-            (blocks, vocab_other, other_flag, post_line, final_line, flag, sampled_line)
-        )
+    blocks, vocab_other, other_flag, flag, sampled_line = lax.optimization_barrier(
+        (blocks, vocab_other, other_flag, flag, sampled_line)
     )
     pieces = exchange(blocks, "tensor")
-    mix = exchange(mix_rows(pieces, residual, post_line), "tensor")
+    mix = exchange(mix_rows(pieces, residual, post_gain), "tensor")
     hidden, new_residual = hidden_blocks(
         mix,
-        final_line,
+        final_gain,
         sampled_line,
         flag,
         other_flag.reshape(1, slot_dev),

time: 103 us -> 101 us (0.981)
  Pallas kernels: 6.5 us -> 16.3 us
  local copies, waits for them, and re-layouts: 6.27 us -> 0.02 us
  matrix products: 4.45 us -> 0 us
    pallas_call x1 -> x2, Pallas kernels: 5.29 us -> 15.1 us  [the longest x1 7.86 us: vocab_stats(): pl.pallas_call(vocab_kernel, in_specs=[*in_vmem(1), hbm, hbm, *in_vmem(1)...]
    dot_general x4 -> x0, matrix products: 4.45 us -> none  [the longest x1 3.13 us: on_device(): jnp.dot(attn, out_weight, preferred_element_type=jnp.float32)]
    reshape x6 -> x0, local copies, waits for them, and re-layouts: 3.19 us -> none  [the longest x2 1.63 us: on_device(): post_line, final_line = (post_gain.reshape(1, D), final_gain.reshape(1, D))]
    unnamed x12 -> x10, local copies, waits for them, and re-layouts: 2.37 us -> 0.02 us
  transfers between devices with their start and end apart: 2 -> 2, of which waited for: 0 -> 1; matrix products, arithmetic and copies ran while one was open for 9% -> 0% of each run, Pallas kernels for 0% -> 7%
where the time goes in v4:
time: 101 us
  blocking collectives  82.1 us (81%)
  Pallas kernels  16.3 us (16%)
    all_to_all x4, blocking collectives, exchange(): return lax.all_to_all(blocks, axes, 0, 0, tiled=True)  82.1 us
    pallas_call x1, Pallas kernels, vocab_stats(): pl.pallas_call(vocab_kernel, in_specs=[*in_vmem(1), hbm, hbm, *in_vmem(1)...  7.86 us
    pallas_call x1, Pallas kernels, attend(): pl.pallas_call(attend_kernel, in_specs=[pl.BlockSpec(memory_space=pltpu.S...  7.21 us
  transfers between devices with their start and end apart: 2, of which 1 were waited for; matrix products, arithmetic and copies ran while one was open for 0% of the time, Pallas kernels for 7%

profile of v4, /device:TPU:8, one launch (start us, length us, event | category | flops | bytes accessed | tf_op | source)
XLA Modules:
  0.0 100.9 jit_solution(13400237102797617243)
XLA Ops:
  0.6 0.0 copy-start.3
  0.6 0.0 copy-start.4
  0.7 0.0 copy-start.1
  0.7 0.0 copy-start
  0.7 0.0 copy-start.2
  0.7 0.1 collective-permute-start
  0.8 0.5 collective-permute-start.1
  1.3 7.2 %attend.1 = bf16[8,2,4608]{2,1,0:T(2,128)(2,1)} custom-call(s32[16]{0:T(128)} %len_ref.1, bf16[16,512]{1,0:T(8,128)(2,1)} %query_hbm.1, bf16[16,256]{1,0:T(8,128)(2,1)} %key_hbm.1, bf16[16,256]{1,0:T(8,128)(2,1)} %value_hbm.1, bf16[16,256,256]{2,1,0:T(8,128)(2,1)} %keys_hbm.1, bf16[16,256,256]{2,1,0:T(8,128)(2,1)} %values_hbm.1, bf16[512,4608]{1,0:T(8,128)(2,1)} %weight_hbm.1), custom_call_target="tpu_custom_call" | custom-call | flops 2000000000 | bytes 9000000 | tf_op jit(solution)/shard_map/attend/pallas_call | solution.py:125
  8.5 0.5 collective-permute-done.1
  9.0 0.0 collective-permute-done.other_hbm
  9.0 18.2 %all_to_all.27.pieces_ref = bf16[8,2,4608]{2,1,0:T(2,128)(2,1)S(1)} all-to-all(bf16[8,2,4608]{2,1,0:T(2,128)(2,1)} %attend.1), channel_id=1, replica_groups=mesh['dp_0'=4,'dp_1'=4,'dp_2'=2,'tensor'=8] {'tensor'}, dimensions={0} | all-to-all | bytes 294912 | tf_op jit(solution)/shard_map/all_to_all | solution.py:154
  27.2 0.0 copy-done.1
  27.2 0.0 copy-done
  27.2 0.2 mix_rows.1
  27.4 11.6 %all_to_all.28.mix_ref = bf16[8,2,4608]{2,1,0:T(2,128)(2,1)S(1)} all-to-all(bf16[8,2,4608]{2,1,0:T(2,128)(2,1)S(1)} %mix_rows.1), channel_id=1, replica_groups=mesh['dp_0'=4,'dp_1'=4,'dp_2'=2,'tensor'=8] {'tensor'}, dimensions={0} | all-to-all | bytes 294912 | tf_op jit(solution)/shard_map/all_to_all | solution.py:154
  39.1 0.0 copy-done.3
  39.1 0.0 copy-done.4
  39.1 0.0 copy-done.2
  39.1 1.0 hidden_blocks.1
  40.1 34.8 %all_to_all.29 = bf16[16,16,4736]{2,1,0:T(8,128)(2,1)S(1)} all-to-all(bf16[16,16,4736]{2,1,0:T(8,128)(2,1)S(1)} %get-tuple-element.19), channel_id=1, replica_groups=mesh['dp_0'=4,'dp_1'=4,'dp_2'=2,'tensor'=8] {'dp_0','dp_1'}, dimensions={0} | all-to-all | bytes 4849664 | tf_op jit(solution)/shard_map/all_to_all | solution.py:154
  74.9 7.9 %vocab_stats.1 = (f32[128,32]{1,0:T(8,128)S(1)}, s32[1,16]{1,0:T(1,128)}, s32[1,1]{1,0:T(1,128)}) custom-call(bf16[256,4736]{1,0:T(8,128)(2,1)S(1)} %bitcast.10, bf16[512,4608]{1,0:T(8,128)(2,1)} %own_hbm.1, bf16[512,4608]{1,0:T(8,128)(2,1)} %collective-permute-done.other_hbm, s32[1,16]{1,0:T(1,128)S(1)} %bitcast.13), custom_call_target="tpu_custom_call" | custom-call | flops 2415919104 | bytes 9437184 | tf_op jit(solution)/shard_map/vocab_stats/pallas_call | solution.py:331
  82.8 17.5 %all_to_all.30 = f32[128,1,32]{2,1,0:T(1,128)S(1)} all-to-all(f32[128,1,32]{2,1,0:T(1,128)S(1)} %bitcast.11), channel_id=1, replica_groups=mesh['dp_0'=4,'dp_1'=4,'dp_2'=2,'tensor'=8] {'dp_0','dp_1','tensor'}, dimensions={0} | all-to-all | bytes 32768 | tf_op jit(solution)/shard_map/all_to_all | solution.py:154
  100.3 0.1 exponential_reduce_fusion
  100.4 0.5 add_subtract_fusion
  (1 shorter events, 0.0 us)
Async XLA Ops:
  0.6 38.4 %copy-start.3 = (s32[16]{0:T(128)S(1)}, s32[16]{0:T(128)}, u32[]{:S(2)}) copy-start(s32[16]{0:T(128)} %param.25) | copy-start | bytes 196
  0.6 38.4 %copy-start.4 = (s32[16]{0:T(128)S(1)}, s32[16]{0:T(128)}, u32[]{:S(2)}) copy-start(s32[16]{0:T(128)} %param.24) | copy-start | bytes 196
  0.7 26.6 %copy-start.1 = (f32[4608]{0:T(1024)S(1)}, f32[4608]{0:T(1024)}, u32[]{:S(2)}) copy-start(f32[4608]{0:T(1024)} %gain_ref.2) | copy-start | bytes 55300
  0.7 26.6 %copy-start = (bf16[16,4608]{1,0:T(8,128)(2,1)S(1)}, bf16[16,4608]{1,0:T(8,128)(2,1)}, u32[]{:S(2)}) copy-start(bf16[16,4608]{1,0:T(8,128)(2,1)} %residual_ref.1) | copy-start | bytes 442372
  0.7 38.4 %copy-start.2 = (f32[4608]{0:T(1024)S(1)}, f32[4608]{0:T(1024)}, u32[]{:S(2)}) copy-start(f32[4608]{0:T(1024)} %gain_ref.3) | copy-start | bytes 55300
  0.7 8.3 %collective-permute-start = (bf16[512,4608]{1,0:T(8,128)(2,1)}, bf16[512,4608]{1,0:T(8,128)(2,1)}, u32[]{:S(2)}, u32[]{:S(2)}) collective-permute-start(bf16[512,4608]{1,0:T(8,128)(2,1)} %own_hbm.1), channel_id=1, source_target_pairs={{0,8},{8,0},{1,9},{9,1},{2,10},{10,2},{3,11},{11,3},{4,12},{12,4},... | collective-permute-start | bytes 14155784 | tf_op jit(solution)/shard_map/ppermute | solution.py:158
  0.8 8.2 %collective-permute-start.1 = (s32[16]{0:T(128)}, s32[16]{0:T(128)S(1)}, u32[]{:S(2)}, u32[]{:S(2)}) collective-permute-start(s32[16]{0:T(128)} %param.25), channel_id=1, source_target_pairs={{0,8},{8,0},{1,9},{9,1},{2,10},{10,2},{3,11},{11,3},{4,12},{12,4},... | collective-permute-start | bytes 200 | tf_op jit(solution)/shard_map/ppermute | solution.py:158

commit v5 on v4

--- a/solution.py
+++ b/solution.py
@@ -15,7 +15,6 @@
 PLANE = ("dp_0", "dp_1")
 CHIPS = ("dp_0", "dp_1", "tensor")
 META = 128
-CHUNKS = 4
 
 
 def attend_kernel(
@@ -212,14 +211,20 @@
     return jnp.sum(jnp.where(row == lane, line, 0), axis=1, keepdims=True)
 
 
-def hidden_kernel(mix_ref, gain_ref, sampled_ref, flag_ref, other_ref, block_ref, slice_ref, rows):
+def hidden_kernel(
+    mix_ref, gain_ref, sampled_ref, flag_ref, other_ref, turn_ref, last_ref, slice_ref, rows
+):
     nz, per, _ = mix_ref.shape
     slot_dev, width = slice_ref.shape
+    third = D // 3
     z = lax.axis_index("tensor")
     for k in range(nz):
         rows[k * per : (k + 1) * per, :] = mix_ref[k].astype(jnp.float32)
     mixed = rows[...]
-    hidden = (mixed * inverse_rms(mixed) * gain_ref[...].reshape(1, D)).astype(jnp.bfloat16)
+    hidden = mixed * inverse_rms(mixed) * gain_ref[...].reshape(1, D)
+    turn = jnp.where(z % 2 == 0, hidden[:, :third], hidden[:, third : 2 * third])
+    turn = turn.astype(jnp.bfloat16)
+    last = hidden[:, 2 * third :].astype(jnp.bfloat16)
     sampled = sampled_ref[...]
     freed = (flag_ref[...] == 1).astype(jnp.int32)
     count = jnp.sum((other_ref[...] == 1).astype(jnp.int32), axis=1, keepdims=True)
@@ -229,9 +234,10 @@
     for k, value in enumerate(values):
         notes = jnp.where(lane == k, as_column(value), notes)
     notes = notes.astype(jnp.float32).astype(jnp.bfloat16)
-    for k in range(block_ref.shape[0]):
-        block_ref[k, :, :D] = hidden
-        block_ref[k, :, D:] = notes
+    for k in range(turn_ref.shape[0]):
+        turn_ref[k] = turn
+        last_ref[k, :, :third] = last
+        last_ref[k, :, third:] = notes
     for k in range(nz):
 
         @pl.when(z == k)
@@ -245,9 +251,10 @@
     return pl.pallas_call(
         hidden_kernel,
         in_specs=in_vmem(5),
-        out_specs=in_vmem(2),
+        out_specs=in_vmem(3),
         out_shape=[
-            jax.ShapeDtypeStruct((planes, slot_dev, D + META), jnp.bfloat16),
+            jax.ShapeDtypeStruct((planes, slot_dev, D // 3), jnp.bfloat16),
+            jax.ShapeDtypeStruct((planes, slot_dev, D // 3 + META), jnp.bfloat16),
             jax.ShapeDtypeStruct((slot_dev, width), jnp.bfloat16),
         ],
         scratch_shapes=[pltpu.VMEM((slot_dev, D), jnp.float32)],
@@ -257,44 +264,40 @@
 
 
 def vocab_kernel(
-    every_ref, own_hbm, other_hbm, flag_ref, pair_ref, rank_ref, total_ref, weights, logits_s, sems
+    turn_ref, before_ref, after_ref, last_ref, notes_ref, own_ref, other_ref, flag_ref,
+    pair_ref, rank_ref, total_ref, every,
 ):
-    slots = every_ref.shape[0]
-    per_device = own_hbm.shape[0]
-    chunk = weights.shape[2]
-    loads = []
-    for k in range(weights.shape[0]):
-        for which, source in enumerate((own_hbm, other_hbm)):
-            copy = pltpu.make_async_copy(
-                source.at[:, pl.ds(k * chunk, chunk)],
-                weights.at[k, pl.ds(which * per_device, per_device)],
-                sems.at[k, which],
-            )
-            copy.start()
-            loads.append(copy)
+    slots = turn_ref.shape[0]
+    per_device = own_ref.shape[0]
+    third = D // 3
     slot_dev = flag_ref.shape[1]
     planes = slots // slot_dev
     nz = pair_ref.shape[0] // planes
     z = lax.axis_index("tensor")
     core = lax.axis_index("dp_2")
     plane = lax.axis_index("dp_0") * lax.axis_size("dp_1") + lax.axis_index("dp_1")
+    for parity in range(2):
+
+        @pl.when(z % 2 == parity)
+        def _():
+            mine, theirs = parity * third, (1 - parity) * third
+            every[:, mine : mine + third] = turn_ref[...]
+            every[:, theirs : theirs + third // 2] = before_ref[...]
+            every[:, theirs + third // 2 : theirs + third] = after_ref[...]
+
+    every[:, 2 * third :] = last_ref[:, :third]
     lane = lax.broadcasted_iota(jnp.int32, (16, META), 1)
     row = lax.broadcasted_iota(jnp.int32, (16, META), 0)
     digit = jnp.where(lane == 0, 1.0, jnp.where(lane == 1, 64.0, jnp.where(lane == 2, 4096.0, 0.0)))
     pick = jnp.where(row == 0, digit, jnp.where(lane == row + 2, 1.0, 0.0))
-    notes = product(pick.astype(jnp.bfloat16), every_ref[:, D:])
+    notes = product(pick.astype(jnp.bfloat16), notes_ref[...])
     ids = notes[0:1, :].astype(jnp.int32)
-    for k in range(weights.shape[0]):
-        loads[2 * k].wait()
-        loads[2 * k + 1].wait()
-        part = product(weights[k], every_ref[:, k * chunk : (k + 1) * chunk])
-        logits_s[...] = part if k == 0 else logits_s[...] + part
     line = lax.broadcasted_iota(jnp.int32, (per_device, slots), 0)
     tops, sums = [], []
     picked = jnp.zeros((1, slots), jnp.float32)
-    for which, holder in enumerate((core, 1 - core)):
+    for rows_ref, holder in ((own_ref, core), (other_ref, 1 - core)):
         begin = ((plane * 2 + holder) * nz + z) * per_device
-        logits = logits_s[which * per_device : (which + 1) * per_device, :]
+        logits = product(rows_ref[...], every[...])
         picked = picked + jnp.sum(jnp.where(line == ids - begin, logits, 0.0), axis=0, keepdims=True)
         top = jnp.max(logits, axis=0, keepdims=True)
         tops.append(top)
@@ -323,31 +326,26 @@
     rank_ref[...] = jnp.where(freed == 1, ahead + before, -1)
 
 
-def vocab_stats(every, own, other, flag, nz):
-    slots = every.shape[0]
+def vocab_stats(turn, before, after, last, notes, own, other, flag, nz):
+    slots = turn.shape[0]
     rows = own.shape[0]
     slot_dev = flag.shape[1]
-    hbm = pl.BlockSpec(memory_space=pltpu.HBM)
     return pl.pallas_call(
         vocab_kernel,
-        in_specs=[*in_vmem(1), hbm, hbm, *in_vmem(1)],
+        in_specs=in_vmem(8),
         out_specs=in_vmem(3),
         out_shape=[
             jax.ShapeDtypeStruct((slots // slot_dev * nz, 2 * slot_dev), jnp.float32),
             jax.ShapeDtypeStruct((1, slot_dev), jnp.int32),
             jax.ShapeDtypeStruct((1, 1), jnp.int32),
         ],
-        scratch_shapes=[
-            pltpu.VMEM((CHUNKS, 2 * rows, D // CHUNKS), jnp.bfloat16),
-            pltpu.VMEM((2 * rows, slots), jnp.float32),
-            pltpu.SemaphoreType.DMA((CHUNKS, 2)),
-        ],
-        compiler_params=params(50),
+        scratch_shapes=[pltpu.VMEM((slots, D), jnp.bfloat16)],
+        compiler_params=params(20),
         cost_estimate=pl.CostEstimate(
             flops=4 * rows * slots * D, bytes_accessed=4 * rows * D, transcendentals=2 * rows * slots
         ),
         name="vocab_stats",
-    )(every, own, other, flag)
+    )(turn, before, after, last, notes, own, other, flag)
 
 
 def on_device(
@@ -368,19 +366,20 @@
     slot_dev = query.shape[0]
     nz = lax.axis_size("tensor")
     planes = lax.axis_size(PLANE)
-    vocab_other = other_core(vocab_weight)
     other_flag = other_core(stop_flag)
-
     blocks = attend(
         query, incoming_key, new_value, key_cache, value_cache, cache_len, out_weight, nz
     )
     flag, sampled_line = stop_flag.reshape(1, slot_dev), sampled.reshape(1, slot_dev)
-    blocks, vocab_other, other_flag, flag, sampled_line = lax.optimization_barrier(
-        (blocks, vocab_other, other_flag, flag, sampled_line)
-    )
+    blocks, vocab_weight, other_flag, flag, sampled_line = lax.optimization_barrier(
+        (blocks, vocab_weight, other_flag, flag, sampled_line)
+    )
+    vocab_other = other_core(vocab_weight)
     pieces = exchange(blocks, "tensor")
     mix = exchange(mix_rows(pieces, residual, post_gain), "tensor")
-    hidden, new_residual = hidden_blocks(
+    mix, vocab_other = lax.optimization_barrier((mix, vocab_other))
+    vocab_own = other_core(vocab_other)
+    turn, last, new_residual = hidden_blocks(
         mix,
         final_gain,
         sampled_line,
@@ -388,8 +387,17 @@
         other_flag.reshape(1, slot_dev),
         planes,
     )
-    every = exchange(hidden, PLANE).reshape(planes * slot_dev, D + META)
-    pair, rank, released = vocab_stats(every, vocab_weight, vocab_other, flag, nz)
+    slots = planes * slot_dev
+    half = D // 6
+    turn = exchange(turn, PLANE).reshape(slots, D // 3)
+    left, right, turn, last = lax.optimization_barrier((turn[:, :half], turn[:, half:], turn, last))
+    before = lax.ppermute(left, "tensor", [(k, (k + 1) % nz) for k in range(nz)])
+    after = lax.ppermute(right, "tensor", [((k + 1) % nz, k) for k in range(nz)])
+    last = exchange(last, PLANE).reshape(slots, D // 3 + META)
+    notes = last[:, D // 3 :]
+    pair, rank, released = vocab_stats(
+        turn, before, after, last, notes, vocab_own, vocab_other, flag, nz
+    )
     gathered = exchange(pair, CHIPS)
     parts = gathered[:, :slot_dev]
     highest = jnp.max(parts, axis=0)

time: 101 us -> 106 us (1.050)
  blocking collectives: 82.1 us -> 69.9 us
  waiting for transfers between devices: 0.53 us -> 9.93 us
  starting transfers between devices: 0.59 us -> 8.96 us
    all_to_all x4, blocking collectives: 82.1 us -> 69.9 us  [exchange(): return lax.all_to_all(blocks, axes, 0, 0, tiled=True)]
    all_to_all x0 -> x1, waiting for transfers between devices: none -> 9.92 us  [exchange(): return lax.all_to_all(blocks, axes, 0, 0, tiled=True)]
    all_to_all x0 -> x1, starting transfers between devices: none -> 5.18 us  [exchange(): return lax.all_to_all(blocks, axes, 0, 0, tiled=True)]
    ppermute x0 -> x2, starting transfers between devices: none -> 3.24 us  [the longest x1 2.63 us: on_device(): lax.ppermute(right, 'tensor', [((k + 1) % nz, k) for k in range(nz)])]
  transfers between devices with their start and end apart: 2 -> 6, of which waited for: 1 -> 1; matrix products, arithmetic and copies ran while one was open for 0% -> 0% of each run, Pallas kernels for 7% -> 8%
where the time goes in v5:
time: 106 us
  blocking collectives  69.9 us (66%)
  Pallas kernels  15.7 us (15%)
  waiting for transfers between devices  9.93 us (9%)
  starting transfers between devices  8.96 us (8%)
    all_to_all x4, blocking collectives, exchange(): return lax.all_to_all(blocks, axes, 0, 0, tiled=True)  69.9 us
    all_to_all x1, waiting for transfers between devices, exchange(): return lax.all_to_all(blocks, axes, 0, 0, tiled=True)  9.92 us
    pallas_call x1, Pallas kernels, attend(): pl.pallas_call(attend_kernel, in_specs=[pl.BlockSpec(memory_space=pltpu.S...  7.37 us
    pallas_call x1, Pallas kernels, vocab_stats(): pl.pallas_call(vocab_kernel, in_specs=in_vmem(8), out_specs=in_vmem(3), o...  6.83 us
    all_to_all x1, starting transfers between devices, exchange(): return lax.all_to_all(blocks, axes, 0, 0, tiled=True)  5.18 us
    ppermute x1, starting transfers between devices, on_device(): lax.ppermute(right, 'tensor', [((k + 1) % nz, k) for k in range(nz)])  2.63 us
  transfers between devices with their start and end apart: 6, of which 1 were waited for; matrix products, arithmetic and copies ran while one was open for 0% of the time, Pallas kernels for 8%

profile of v5, /device:TPU:8, one launch (start us, length us, event | category | flops | bytes accessed | tf_op | source)
XLA Modules:
  0.0 106.0 jit_solution(16540389717332140796)
XLA Ops:
  0.6 0.0 copy-start.3
  0.6 0.0 copy-start.4
  0.7 0.0 copy-start.1
  0.7 0.0 copy-start
  0.7 0.0 copy-start.2
  0.7 0.1 collective-permute-start
  0.8 7.4 %attend.1 = bf16[8,2,4608]{2,1,0:T(2,128)(2,1)} custom-call(s32[16]{0:T(128)} %len_ref.1, bf16[16,512]{1,0:T(8,128)(2,1)} %query_hbm.1, bf16[16,256]{1,0:T(8,128)(2,1)} %key_hbm.1, bf16[16,256]{1,0:T(8,128)(2,1)} %value_hbm.1, bf16[16,256,256]{2,1,0:T(8,128)(2,1)} %keys_hbm.1, bf16[16,256,256]{2,1,0:T(8,128)(2,1)} %values_hbm.1, bf16[512,4608]{1,0:T(8,128)(2,1)} %weight_hbm.1), custom_call_target="tpu_custom_call" | custom-call | flops 2000000000 | bytes 9000000 | tf_op jit(solution)/shard_map/attend/pallas_call | solution.py:124
  8.2 0.0 collective-permute-done
  8.2 0.5 collective-permute-start.1
  8.6 18.2 %all_to_all.32.pieces_ref = bf16[8,2,4608]{2,1,0:T(2,128)(2,1)S(1)} all-to-all(bf16[8,2,4608]{2,1,0:T(2,128)(2,1)} %attend.1), channel_id=1, replica_groups=mesh['dp_0'=4,'dp_1'=4,'dp_2'=2,'tensor'=8] {'tensor'}, dimensions={0} | all-to-all | bytes 294912 | tf_op jit(solution)/shard_map/all_to_all | solution.py:153
  26.8 0.0 copy-done.1
  26.8 0.0 copy-done
  26.8 0.2 mix_rows.1
  27.0 11.6 %all_to_all.33.mix_ref = bf16[8,2,4608]{2,1,0:T(2,128)(2,1)S(1)} all-to-all(bf16[8,2,4608]{2,1,0:T(2,128)(2,1)S(1)} %mix_rows.1), channel_id=1, replica_groups=mesh['dp_0'=4,'dp_1'=4,'dp_2'=2,'tensor'=8] {'tensor'}, dimensions={0} | all-to-all | bytes 294912 | tf_op jit(solution)/shard_map/all_to_all | solution.py:153
  38.7 0.0 collective-permute-done.1.other_ref
  38.7 0.0 collective-permute-start.4
  38.7 0.0 copy-done.3
  38.7 0.0 copy-done.4
  38.7 0.0 copy-done.2
  38.7 1.3 %hidden_blocks.1 = (bf16[16,16,1536]{2,1,0:T(8,128)(2,1)S(1)}, bf16[16,16,1664]{2,1,0:T(8,128)(2,1)}, bf16[16,576]{1,0:T(8,128)(2,1)}) custom-call(bf16[8,2,4608]{2,1,0:T(2,128)(2,1)S(1)} %all_to_all.33.mix_ref, f32[4608]{0:T(1024)S(1)} %copy-done.2, s32[1,16]{1,0:T(1,128)S(1)} %bitcast.18, s32[1,16]{1,0:T(1,128)S(1)} %bitcast.16, s32[1,16]{1,0:T(1,128)S(1)} %bitcast.19), custom_call_target="tpu_custom_call" | custom-call | tf_op jit(solution)/shard_map/hidden_blocks/pallas_call | solution.py:251
  40.0 20.4 %all_to_all.34 = bf16[16,16,1536]{2,1,0:T(8,128)(2,1)S(1)} all-to-all(bf16[16,16,1536]{2,1,0:T(8,128)(2,1)S(1)} %get-tuple-element.28), channel_id=1, replica_groups=mesh['dp_0'=4,'dp_1'=4,'dp_2'=2,'tensor'=8] {'dp_0','dp_1'}, dimensions={0} | all-to-all | bytes 1572864 | tf_op jit(solution)/shard_map/all_to_all | solution.py:153
  60.4 0.1 fusion
  60.4 5.2 %all-to-all-start.3 = ((bf16[16,16,1664]{2,1,0:T(8,128)(2,1)}), bf16[16,16,1664]{2,1,0:T(8,128)(2,1)S(1)}, u32[]{:S(2)}, u32[]{:S(2)}) async-start(bf16[16,16,1664]{2,1,0:T(8,128)(2,1)} %get-tuple-element.33), calls=%async_computation.3 | async-start | bytes 1703936 | tf_op jit(solution)/shard_map/all_to_all | solution.py:153
  65.6 0.6 collective-permute-start.2
  66.2 2.6 %collective-permute-start.3 = (bf16[256,768]{1,0:T(8,128)(2,1)S(1)}, bf16[256,768]{1,0:T(8,128)(2,1)S(1)}, u32[]{:S(2)}, u32[]{:S(2)}) collective-permute-start(bf16[256,768]{1,0:T(8,128)(2,1)S(1)} %get-tuple-element.32), channel_id=1, source_target_pairs={{1,0},{2,1},{3,2},{4,3},{5,4},{6,5},{7,6},{0,7},{9,8},{10,9},{11,1... | collective-permute-start | bytes 1179656 | tf_op jit(solution)/shard_map/ppermute | solution.py:395
  68.9 9.9 %all-to-all-done.3 = bf16[16,16,1664]{2,1,0:T(8,128)(2,1)S(1)} async-done(((bf16[16,16,1664]{2,1,0:T(8,128)(2,1)}), bf16[16,16,1664]{2,1,0:T(8,128)(2,1)S(1)}, u32[]{:S(2)}, u32[]{:S(2)}) %all-to-all-start.3) | async-done | bytes 852000 | tf_op jit(solution)/shard_map/all_to_all | solution.py:153
  78.8 0.0 collective-permute-done.2.before_ref
  78.8 0.0 collective-permute-done.3.after_ref
  78.8 0.0 collective-permute-done.4.own_ref
  78.8 6.8 %vocab_stats.1 = (f32[128,32]{1,0:T(8,128)S(1)}, s32[1,16]{1,0:T(1,128)}, s32[1,1]{1,0:T(1,128)}) custom-call(bf16[256,1536]{1,0:T(8,128)(2,1)S(1)} %bitcast.12, bf16[256,768]{1,0:T(8,128)(2,1)S(1)} %collective-permute-done.2.before_ref, bf16[256,768]{1,0:T(8,128)(2,1)S(1)} %collective-permute-done.3.after_ref, bf16[256,1664]{1,0:T(8,128)(2,1)S(1)} %bitcast.14, ...), custom_call_target="tpu_custom_call" | custom-call | flops 2415919104 | bytes 9437184 | tf_op jit(solution)/shard_map/vocab_stats/pallas_call | solution.py:333
  85.6 19.7 %all_to_all.35 = f32[128,1,32]{2,1,0:T(1,128)S(1)} all-to-all(f32[128,1,32]{2,1,0:T(1,128)S(1)} %bitcast.15), channel_id=1, replica_groups=mesh['dp_0'=4,'dp_1'=4,'dp_2'=2,'tensor'=8] {'dp_0','dp_1','tensor'}, dimensions={0} | all-to-all | bytes 32768 | tf_op jit(solution)/shard_map/all_to_all | solution.py:153
  105.4 0.1 exponential_reduce_fusion
  105.5 0.5 add_subtract_fusion
  (2 shorter events, 0.0 us)
Async XLA Ops:
  0.6 38.0 %copy-start.3 = (s32[16]{0:T(128)S(1)}, s32[16]{0:T(128)}, u32[]{:S(2)}) copy-start(s32[16]{0:T(128)} %param.25) | copy-start | bytes 196
  0.6 38.0 %copy-start.4 = (s32[16]{0:T(128)S(1)}, s32[16]{0:T(128)}, u32[]{:S(2)}) copy-start(s32[16]{0:T(128)} %param.24) | copy-start | bytes 196
  0.7 26.2 %copy-start.1 = (f32[4608]{0:T(1024)S(1)}, f32[4608]{0:T(1024)}, u32[]{:S(2)}) copy-start(f32[4608]{0:T(1024)} %gain_ref.2) | copy-start | bytes 55300
  0.7 26.2 %copy-start = (bf16[16,4608]{1,0:T(8,128)(2,1)S(1)}, bf16[16,4608]{1,0:T(8,128)(2,1)}, u32[]{:S(2)}) copy-start(bf16[16,4608]{1,0:T(8,128)(2,1)} %residual_ref.1) | copy-start | bytes 442372
  0.7 38.0 %copy-start.2 = (f32[4608]{0:T(1024)S(1)}, f32[4608]{0:T(1024)}, u32[]{:S(2)}) copy-start(f32[4608]{0:T(1024)} %gain_ref.3) | copy-start | bytes 55300
  0.7 7.5 %collective-permute-start = (s32[16]{0:T(128)}, s32[16]{0:T(128)S(1)}, u32[]{:S(2)}, u32[]{:S(2)}) collective-permute-start(s32[16]{0:T(128)} %param.25), channel_id=1, source_target_pairs={{0,8},{8,0},{1,9},{9,1},{2,10},{10,2},{3,11},{11,3},{4,12},{12,4},... | collective-permute-start | bytes 200 | tf_op jit(solution)/shard_map/ppermute | solution.py:157
  8.2 30.5 %collective-permute-start.1 = (bf16[512,4608]{1,0:T(8,128)(2,1)}, bf16[512,4608]{1,0:T(8,128)(2,1)}, u32[]{:S(2)}, u32[]{:S(2)}) collective-permute-start(bf16[512,4608]{1,0:T(8,128)(2,1)} %param.23), channel_id=1, source_target_pairs={{0,8},{8,0},{1,9},{9,1},{2,10},{10,2},{3,11},{11,3},{4,12},{12,4},... | collective-permute-start | bytes 14155784 | tf_op jit(solution)/shard_map/ppermute | solution.py:157
  38.7 40.1 %collective-permute-start.4 = (bf16[512,4608]{1,0:T(8,128)(2,1)}, bf16[512,4608]{1,0:T(8,128)(2,1)}, u32[]{:S(2)}, u32[]{:S(2)}) collective-permute-start(bf16[512,4608]{1,0:T(8,128)(2,1)} %collective-permute-done.1.other_ref), channel_id=1, source_target_pairs={{0,8},{8,0},{1,9},{9,1},{2,10},{10,2},{3,11},{11,3},{4,12},{12,4},... | collective-permute-start | bytes 14155784 | tf_op jit(solution)/shard_map/ppermute | solution.py:157
  60.4 18.3 %all-to-all-start.3 = ((bf16[16,16,1664]{2,1,0:T(8,128)(2,1)}), bf16[16,16,1664]{2,1,0:T(8,128)(2,1)S(1)}, u32[]{:S(2)}, u32[]{:S(2)}) async-start(bf16[16,16,1664]{2,1,0:T(8,128)(2,1)} %get-tuple-element.33), calls=%async_computation.3 | async-start | bytes 1703936 | tf_op jit(solution)/shard_map/all_to_all | solution.py:153
  65.6 13.2 %collective-permute-start.2 = (bf16[256,768]{1,0:T(8,128)(2,1)S(1)}, bf16[256,768]{1,0:T(8,128)(2,1)S(1)}, u32[]{:S(2)}, u32[]{:S(2)}) collective-permute-start(bf16[256,768]{1,0:T(8,128)(2,1)S(1)} %get-tuple-element.31), channel_id=1, source_target_pairs={{0,1},{1,2},{2,3},{3,4},{4,5},{5,6},{6,7},{7,0},{8,9},{9,10},{10,1... | collective-permute-start | bytes 1179656 | tf_op jit(solution)/shard_map/ppermute | solution.py:394
  66.2 12.6 %collective-permute-start.3 = (bf16[256,768]{1,0:T(8,128)(2,1)S(1)}, bf16[256,768]{1,0:T(8,128)(2,1)S(1)}, u32[]{:S(2)}, u32[]{:S(2)}) collective-permute-start(bf16[256,768]{1,0:T(8,128)(2,1)S(1)} %get-tuple-element.32), channel_id=1, source_target_pairs={{1,0},{2,1},{3,2},{4,3},{5,4},{6,5},{7,6},{0,7},{9,8},{10,9},{11,1... | collective-permute-start | bytes 1179656 | tf_op jit(solution)/shard_map/ppermute | solution.py:395

commit v6 on v4

--- a/solution.py
+++ b/solution.py
@@ -15,13 +15,12 @@
 PLANE = ("dp_0", "dp_1")
 CHIPS = ("dp_0", "dp_1", "tensor")
 META = 128
-CHUNKS = 4
 
 
 def attend_kernel(
     len_ref, query_hbm, key_hbm, value_hbm, keys_hbm, values_hbm, weight_hbm, out_hbm,
     keys, values, weight, query_ref, key_ref, value_ref, out_ref,
-    query_s, key_s, value_s, score_s, attn_s, part_s, key_sem, value_sem, weight_sem, small_sem,
+    query_s, key_s, value_s, score_s, attn_s, key_sem, value_sem, weight_sem, small_sem, out_sem,
 ):
     slot_dev = keys.shape[0]
     positions = keys.shape[1]
@@ -45,7 +44,6 @@
         loads["w", k] = pltpu.make_async_copy(
             weight_hbm.at[:, part], weight.at[:, part], weight_sem.at[k]
         )
-        loads["w", k].start()
 
     for k in range(len(smalls)):
         loads["s", k].wait()
@@ -77,6 +75,8 @@
         spread = [jnp.where(kind == k, rows, 0.0) for k in range(kv_local)]
         spread = jnp.concatenate(spread, axis=1).astype(jnp.bfloat16)
         score_s[i * lines : (i + 1) * lines, :] = per_slot(spread, keys, i * pair, 1)
+        if (i + 1) * pair % batch == 0:
+            loads["w", i * pair // batch].start()
 
     total_rows = slot_dev * heads
     owner = lax.broadcasted_iota(jnp.int32, (total_rows, 1), 0) // heads
@@ -105,17 +105,21 @@
     attn_s[...] += own_weight * value_s[...]
     attn = [attn_s[pl.ds(h, slot_dev, stride=heads), :] for h in range(heads)]
     attn = jnp.concatenate(attn, axis=1).astype(jnp.bfloat16)
+    per = out_ref.shape[1]
+    stores = []
     for k in range(weight_sem.shape[0]):
         loads["w", k].wait()
-        part_s[:, k * chunk : (k + 1) * chunk] = jnp.dot(
-            attn, weight[:, k * chunk : (k + 1) * chunk], preferred_element_type=jnp.float32
+        columns = slice(k * chunk, (k + 1) * chunk)
+        part = jnp.dot(attn, weight[:, columns], preferred_element_type=jnp.float32)
+        for p in range(out_ref.shape[0]):
+            out_ref[p, :, columns] = part[p * per : (p + 1) * per, :].astype(jnp.bfloat16)
+        where = pl.ds(k * chunk, chunk)
+        stores.append(
+            pltpu.make_async_copy(out_ref.at[:, :, where], out_hbm.at[:, :, where], out_sem.at[k])
         )
-    per = out_ref.shape[1]
-    for k in range(out_ref.shape[0]):
-        out_ref[k] = part_s[k * per : (k + 1) * per, :].astype(jnp.bfloat16)
-    store = pltpu.make_async_copy(out_ref, out_hbm, small_sem.at[0])
-    store.start()
-    store.wait()
+        stores[-1].start()
+    for store in stores:
+        store.wait()
 
 
 def attend(query, incoming_key, new_value, key_cache, value_cache, cache_len, out_weight, nz):
@@ -138,11 +142,11 @@
             *[pltpu.VMEM((lines, HEAD_DIM), jnp.float32)] * 3,
             pltpu.VMEM((lines, key_cache.shape[1]), jnp.float32),
             pltpu.VMEM((lines, HEAD_DIM), jnp.float32),
-            pltpu.VMEM((slot_dev, D), jnp.float32),
             pltpu.SemaphoreType.DMA((4,)),
             pltpu.SemaphoreType.DMA((4,)),
             pltpu.SemaphoreType.DMA((4,)),
             pltpu.SemaphoreType.DMA((3,)),
+            pltpu.SemaphoreType.DMA((4,)),
         ],
         compiler_params=params(61),
         cost_estimate=pl.CostEstimate(flops=2_000_000_000, bytes_accessed=9_000_000, transcendentals=20_000),
@@ -257,21 +261,10 @@
 
 
 def vocab_kernel(
-    every_ref, own_hbm, other_hbm, flag_ref, pair_ref, rank_ref, total_ref, weights, logits_s, sems
+    every_ref, own_ref, other_ref, flag_ref, pair_ref, rank_ref, total_ref
 ):
     slots = every_ref.shape[0]
-    per_device = own_hbm.shape[0]
-    chunk = weights.shape[2]
-    loads = []
-    for k in range(weights.shape[0]):
-        for which, source in enumerate((own_hbm, other_hbm)):
-            copy = pltpu.make_async_copy(
-                source.at[:, pl.ds(k * chunk, chunk)],
-                weights.at[k, pl.ds(which * per_device, per_device)],
-                sems.at[k, which],
-            )
-            copy.start()
-            loads.append(copy)
+    per_device = own_ref.shape[0]
     slot_dev = flag_ref.shape[1]
     planes = slots // slot_dev
     nz = pair_ref.shape[0] // planes
@@ -284,17 +277,12 @@
     pick = jnp.where(row == 0, digit, jnp.where(lane == row + 2, 1.0, 0.0))
     notes = product(pick.astype(jnp.bfloat16), every_ref[:, D:])
     ids = notes[0:1, :].astype(jnp.int32)
-    for k in range(weights.shape[0]):
-        loads[2 * k].wait()
-        loads[2 * k + 1].wait()
-        part = product(weights[k], every_ref[:, k * chunk : (k + 1) * chunk])
-        logits_s[...] = part if k == 0 else logits_s[...] + part
     line = lax.broadcasted_iota(jnp.int32, (per_device, slots), 0)
     tops, sums = [], []
     picked = jnp.zeros((1, slots), jnp.float32)
-    for which, holder in enumerate((core, 1 - core)):
+    for rows_ref, holder in ((own_ref, core), (other_ref, 1 - core)):
         begin = ((plane * 2 + holder) * nz + z) * per_device
-        logits = logits_s[which * per_device : (which + 1) * per_device, :]
+        logits = product(rows_ref[...], every_ref[:, :D])
         picked = picked + jnp.sum(jnp.where(line == ids - begin, logits, 0.0), axis=0, keepdims=True)
         top = jnp.max(logits, axis=0, keepdims=True)
         tops.append(top)
@@ -327,22 +315,16 @@
     slots = every.shape[0]
     rows = own.shape[0]
     slot_dev = flag.shape[1]
-    hbm = pl.BlockSpec(memory_space=pltpu.HBM)
     return pl.pallas_call(
         vocab_kernel,
-        in_specs=[*in_vmem(1), hbm, hbm, *in_vmem(1)],
+        in_specs=in_vmem(4),
         out_specs=in_vmem(3),
         out_shape=[
             jax.ShapeDtypeStruct((slots // slot_dev * nz, 2 * slot_dev), jnp.float32),
             jax.ShapeDtypeStruct((1, slot_dev), jnp.int32),
             jax.ShapeDtypeStruct((1, 1), jnp.int32),
         ],
-        scratch_shapes=[
-            pltpu.VMEM((CHUNKS, 2 * rows, D // CHUNKS), jnp.bfloat16),
-            pltpu.VMEM((2 * rows, slots), jnp.float32),
-            pltpu.SemaphoreType.DMA((CHUNKS, 2)),
-        ],
-        compiler_params=params(50),
+        compiler_params=params(20),
         cost_estimate=pl.CostEstimate(
             flops=4 * rows * slots * D, bytes_accessed=4 * rows * D, transcendentals=2 * rows * slots
         ),
@@ -368,16 +350,16 @@
     slot_dev = query.shape[0]
     nz = lax.axis_size("tensor")
     planes = lax.axis_size(PLANE)
-    vocab_other = other_core(vocab_weight)
     other_flag = other_core(stop_flag)
 
     blocks = attend(
         query, incoming_key, new_value, key_cache, value_cache, cache_len, out_weight, nz
     )
     flag, sampled_line = stop_flag.reshape(1, slot_dev), sampled.reshape(1, slot_dev)
-    blocks, vocab_other, other_flag, flag, sampled_line = lax.optimization_barrier(
-        (blocks, vocab_other, other_flag, flag, sampled_line)
-    )
+    blocks, vocab_weight, other_flag, flag, sampled_line = lax.optimization_barrier(
+        (blocks, vocab_weight, other_flag, flag, sampled_line)
+    )
+    vocab_other = other_core(vocab_weight)
     pieces = exchange(blocks, "tensor")
     mix = exchange(mix_rows(pieces, residual, post_gain), "tensor")
     hidden, new_residual = hidden_blocks(

time: 101 us -> 95.1 us (0.942)
  Pallas kernels: 16.3 us -> 10.4 us
    pallas_call x1, Pallas kernels: 7.86 us -> 2.95 us  [vocab_stats(): pl.pallas_call(vocab_kernel, in_specs=in_vmem(4), out_specs=in_vmem(3), o...]
  transfers between devices with their start and end apart: 2 -> 2, of which waited for: 1 -> 0; matrix products, arithmetic and copies ran while one was open for 0% -> 0% of each run, Pallas kernels for 7% -> 8%
where the time goes in v6:
time: 95.1 us; the launch traced here: 94.8 us
  blocking collectives  82.4 us (87%)
  Pallas kernels  10.4 us (11%)
    all_to_all x4, blocking collectives, exchange(): return lax.all_to_all(blocks, axes, 0, 0, tiled=True)  82.4 us
    pallas_call x1, Pallas kernels, attend(): pl.pallas_call(attend_kernel, in_specs=[pl.BlockSpec(memory_space=pltpu.S...  6.29 us
    pallas_call x1, Pallas kernels, vocab_stats(): pl.pallas_call(vocab_kernel, in_specs=in_vmem(4), out_specs=in_vmem(3), o...  2.95 us
  transfers between devices with their start and end apart: 2, of which 0 were waited for; matrix products, arithmetic and copies ran while one was open for 0% of the time, Pallas kernels for 8%

profile of v6, /device:TPU:8, one launch (start us, length us, event | category | flops | bytes accessed | tf_op | source)
XLA Modules:
  0.0 94.8 jit_solution(13832252240618057571)
XLA Ops:
  0.6 0.0 copy-start.4
  0.6 0.0 copy-start.5
  0.7 0.0 copy-start.2
  0.7 0.0 copy-start.1
  0.7 0.0 copy-start.3
  0.7 0.1 collective-permute-start
  0.8 6.3 %attend.1 = bf16[8,2,4608]{2,1,0:T(2,128)(2,1)} custom-call(s32[16]{0:T(128)} %len_ref.1, bf16[16,512]{1,0:T(8,128)(2,1)} %query_hbm.1, bf16[16,256]{1,0:T(8,128)(2,1)} %key_hbm.1, bf16[16,256]{1,0:T(8,128)(2,1)} %value_hbm.1, bf16[16,256,256]{2,1,0:T(8,128)(2,1)} %keys_hbm.1, bf16[16,256,256]{2,1,0:T(8,128)(2,1)} %values_hbm.1, bf16[512,4608]{1,0:T(8,128)(2,1)} %weight_hbm.1), custom_call_target="tpu_custom_call" | custom-call | flops 2000000000 | bytes 9000000 | tf_op jit(solution)/shard_map/attend/pallas_call | solution.py:129
  7.1 0.0 collective-permute-done
  7.1 0.5 collective-permute-start.1
  7.5 18.2 %all_to_all.27.pieces_ref = bf16[8,2,4608]{2,1,0:T(2,128)(2,1)S(1)} all-to-all(bf16[8,2,4608]{2,1,0:T(2,128)(2,1)} %attend.1), channel_id=1, replica_groups=mesh['dp_0'=4,'dp_1'=4,'dp_2'=2,'tensor'=8] {'tensor'}, dimensions={0} | all-to-all | bytes 294912 | tf_op jit(solution)/shard_map/all_to_all | solution.py:158
  25.7 0.0 copy-done.2
  25.7 0.0 copy-done.1
  25.7 0.2 mix_rows.1
  26.0 11.6 %all_to_all.28.mix_ref = bf16[8,2,4608]{2,1,0:T(2,128)(2,1)S(1)} all-to-all(bf16[8,2,4608]{2,1,0:T(2,128)(2,1)S(1)} %mix_rows.1), channel_id=1, replica_groups=mesh['dp_0'=4,'dp_1'=4,'dp_2'=2,'tensor'=8] {'tensor'}, dimensions={0} | all-to-all | bytes 294912 | tf_op jit(solution)/shard_map/all_to_all | solution.py:158
  37.6 0.0 copy-done.4
  37.6 0.0 copy-done.5
  37.6 0.0 copy-done.3
  37.6 1.0 %hidden_blocks.1 = (bf16[16,16,4736]{2,1,0:T(8,128)(2,1)S(1)}, bf16[16,576]{1,0:T(8,128)(2,1)}) custom-call(bf16[8,2,4608]{2,1,0:T(2,128)(2,1)S(1)} %all_to_all.28.mix_ref, f32[4608]{0:T(1024)S(1)} %copy-done.3, s32[1,16]{1,0:T(1,128)S(1)} %bitcast.14, s32[1,16]{1,0:T(1,128)S(1)} %bitcast.12, s32[1,16]{1,0:T(1,128)S(1)} %bitcast.15), custom_call_target="tpu_custom_call" | custom-call | tf_op jit(solution)/shard_map/hidden_blocks/pallas_call | solution.py:249
  38.6 0.0 copy-start
  38.6 35.1 %all_to_all.29 = bf16[16,16,4736]{2,1,0:T(8,128)(2,1)S(1)} all-to-all(bf16[16,16,4736]{2,1,0:T(8,128)(2,1)S(1)} %get-tuple-element.19), channel_id=1, replica_groups=mesh['dp_0'=4,'dp_1'=4,'dp_2'=2,'tensor'=8] {'dp_0','dp_1'}, dimensions={0} | all-to-all | bytes 4849664 | tf_op jit(solution)/shard_map/all_to_all | solution.py:158
  73.7 0.0 collective-permute-done.1.other_ref
  73.7 0.0 copy-done
  73.7 3.0 %vocab_stats.1 = (f32[128,32]{1,0:T(8,128)S(1)}, s32[1,16]{1,0:T(1,128)}, s32[1,1]{1,0:T(1,128)}) custom-call(bf16[256,4736]{1,0:T(8,128)(2,1)S(1)} %bitcast.10, bf16[512,4608]{1,0:T(8,128)(2,1)S(1)} %copy-done, bf16[512,4608]{1,0:T(8,128)(2,1)S(1)} %collective-permute-done.1.other_ref, s32[1,16]{1,0:T(1,128)S(1)} %bitcast.13), custom_call_target="tpu_custom_call" | custom-call | flops 2415919104 | bytes 9437184 | tf_op jit(solution)/shard_map/vocab_stats/pallas_call | solution.py:318
  76.7 17.5 %all_to_all.30 = f32[128,1,32]{2,1,0:T(1,128)S(1)} all-to-all(f32[128,1,32]{2,1,0:T(1,128)S(1)} %bitcast.11), channel_id=1, replica_groups=mesh['dp_0'=4,'dp_1'=4,'dp_2'=2,'tensor'=8] {'dp_0','dp_1','tensor'}, dimensions={0} | all-to-all | bytes 32768 | tf_op jit(solution)/shard_map/all_to_all | solution.py:158
  94.2 0.1 exponential_reduce_fusion
  94.3 0.5 add_subtract_fusion
  (1 shorter events, 0.0 us)
Async XLA Ops:
  0.6 37.0 %copy-start.4 = (s32[16]{0:T(128)S(1)}, s32[16]{0:T(128)}, u32[]{:S(2)}) copy-start(s32[16]{0:T(128)} %param.25) | copy-start | bytes 196
  0.6 37.0 %copy-start.5 = (s32[16]{0:T(128)S(1)}, s32[16]{0:T(128)}, u32[]{:S(2)}) copy-start(s32[16]{0:T(128)} %param.24) | copy-start | bytes 196
  0.7 25.1 %copy-start.2 = (f32[4608]{0:T(1024)S(1)}, f32[4608]{0:T(1024)}, u32[]{:S(2)}) copy-start(f32[4608]{0:T(1024)} %gain_ref.2) | copy-start | bytes 55300
  0.7 25.1 %copy-start.1 = (bf16[16,4608]{1,0:T(8,128)(2,1)S(1)}, bf16[16,4608]{1,0:T(8,128)(2,1)}, u32[]{:S(2)}) copy-start(bf16[16,4608]{1,0:T(8,128)(2,1)} %residual_ref.1) | copy-start | bytes 442372
  0.7 36.9 %copy-start.3 = (f32[4608]{0:T(1024)S(1)}, f32[4608]{0:T(1024)}, u32[]{:S(2)}) copy-start(f32[4608]{0:T(1024)} %gain_ref.3) | copy-start | bytes 55300
  0.7 6.4 %collective-permute-start = (s32[16]{0:T(128)}, s32[16]{0:T(128)S(1)}, u32[]{:S(2)}, u32[]{:S(2)}) collective-permute-start(s32[16]{0:T(128)} %param.25), channel_id=1, source_target_pairs={{0,8},{8,0},{1,9},{9,1},{2,10},{10,2},{3,11},{11,3},{4,12},{12,4},... | collective-permute-start | bytes 200 | tf_op jit(solution)/shard_map/ppermute | solution.py:162
  7.1 66.6 %collective-permute-start.1 = (bf16[512,4608]{1,0:T(8,128)(2,1)}, bf16[512,4608]{1,0:T(8,128)(2,1)S(1)}, u32[]{:S(2)}, u32[]{:S(2)}) collective-permute-start(bf16[512,4608]{1,0:T(8,128)(2,1)} %own_ref), channel_id=1, source_target_pairs={{0,8},{8,0},{1,9},{9,1},{2,10},{10,2},{3,11},{11,3},{4,12},{12,4},... | collective-permute-start | bytes 14155784 | tf_op jit(solution)/shard_map/ppermute | solution.py:162
  38.6 35.1 %copy-start = (bf16[512,4608]{1,0:T(8,128)(2,1)S(1)}, bf16[512,4608]{1,0:T(8,128)(2,1)}, u32[]{:S(2)}) copy-start(bf16[512,4608]{1,0:T(8,128)(2,1)} %own_ref) | copy-start | bytes 14155780

commit v7 on v6

--- a/solution.py
+++ b/solution.py
@@ -29,6 +29,7 @@
     kv_local = heads // group
     batch = slot_dev // key_sem.shape[0]
     chunk = D // weight_sem.shape[0]
+    pace = slot_dev // weight_sem.shape[0]
     loads = {}
     smalls = ((query_hbm, query_ref), (key_hbm, key_ref), (value_hbm, value_ref))
     for k, (source, target) in enumerate(smalls):
@@ -75,8 +76,8 @@
         spread = [jnp.where(kind == k, rows, 0.0) for k in range(kv_local)]
         spread = jnp.concatenate(spread, axis=1).astype(jnp.bfloat16)
         score_s[i * lines : (i + 1) * lines, :] = per_slot(spread, keys, i * pair, 1)
-        if (i + 1) * pair % batch == 0:
-            loads["w", i * pair // batch].start()
+        if (i + 1) * pair % pace == 0:
+            loads["w", i * pair // pace].start()
 
     total_rows = slot_dev * heads
     owner = lax.broadcasted_iota(jnp.int32, (total_rows, 1), 0) // heads
@@ -142,8 +143,8 @@
             *[pltpu.VMEM((lines, HEAD_DIM), jnp.float32)] * 3,
             pltpu.VMEM((lines, key_cache.shape[1]), jnp.float32),
             pltpu.VMEM((lines, HEAD_DIM), jnp.float32),
-            pltpu.SemaphoreType.DMA((4,)),
-            pltpu.SemaphoreType.DMA((4,)),
+            pltpu.SemaphoreType.DMA((8,)),
+            pltpu.SemaphoreType.DMA((8,)),
             pltpu.SemaphoreType.DMA((4,)),
             pltpu.SemaphoreType.DMA((3,)),
             pltpu.SemaphoreType.DMA((4,)),

time: 95.1 us -> 96.2 us (1.012)
  Pallas kernels: 10.4 us -> 11.6 us
    pallas_call x1, Pallas kernels: 6.29 us -> 7.45 us  [attend(): pl.pallas_call(attend_kernel, in_specs=[pl.BlockSpec(memory_space=pltpu.S...]
  transfers between devices with their start and end apart: 2 -> 2, of which waited for: 0 -> 0; matrix products, arithmetic and copies ran while one was open for 0% -> 0% of each run, Pallas kernels for 8% -> 9%
where the time goes in v7:
time: 96.2 us; the launch traced here: 96 us
  blocking collectives  82.4 us (86%)
  Pallas kernels  11.6 us (12%)
    all_to_all x4, blocking collectives, exchange(): return lax.all_to_all(blocks, axes, 0, 0, tiled=True)  82.4 us
    pallas_call x1, Pallas kernels, attend(): pl.pallas_call(attend_kernel, in_specs=[pl.BlockSpec(memory_space=pltpu.S...  7.45 us
    pallas_call x1, Pallas kernels, vocab_stats(): pl.pallas_call(vocab_kernel, in_specs=in_vmem(4), out_specs=in_vmem(3), o...  2.96 us
  transfers between devices with their start and end apart: 2, of which 0 were waited for; matrix products, arithmetic and copies ran while one was open for 0% of the time, Pallas kernels for 9%

profile of v7, /device:TPU:8, one launch (start us, length us, event | category | flops | bytes accessed | tf_op | source)
XLA Modules:
  0.0 96.0 jit_solution(12334002320656400547)
XLA Ops:
  0.6 0.0 copy-start.4
  0.6 0.0 copy-start.5
  0.7 0.0 copy-start.2
  0.7 0.0 copy-start.1
  0.7 0.0 copy-start.3
  0.7 0.1 collective-permute-start
  0.8 7.4 %attend.1 = bf16[8,2,4608]{2,1,0:T(2,128)(2,1)} custom-call(s32[16]{0:T(128)} %len_ref.1, bf16[16,512]{1,0:T(8,128)(2,1)} %query_hbm.1, bf16[16,256]{1,0:T(8,128)(2,1)} %key_hbm.1, bf16[16,256]{1,0:T(8,128)(2,1)} %value_hbm.1, bf16[16,256,256]{2,1,0:T(8,128)(2,1)} %keys_hbm.1, bf16[16,256,256]{2,1,0:T(8,128)(2,1)} %values_hbm.1, bf16[512,4608]{1,0:T(8,128)(2,1)} %weight_hbm.1), custom_call_target="tpu_custom_call" | custom-call | flops 2000000000 | bytes 9000000 | tf_op jit(solution)/shard_map/attend/pallas_call | solution.py:130
  8.2 0.0 collective-permute-done
  8.2 0.5 collective-permute-start.1
  8.7 18.2 %all_to_all.27.pieces_ref = bf16[8,2,4608]{2,1,0:T(2,128)(2,1)S(1)} all-to-all(bf16[8,2,4608]{2,1,0:T(2,128)(2,1)} %attend.1), channel_id=1, replica_groups=mesh['dp_0'=4,'dp_1'=4,'dp_2'=2,'tensor'=8] {'tensor'}, dimensions={0} | all-to-all | bytes 294912 | tf_op jit(solution)/shard_map/all_to_all | solution.py:159
  26.9 0.0 copy-done.2
  26.9 0.0 copy-done.1
  26.9 0.2 mix_rows.1
  27.1 11.6 %all_to_all.28.mix_ref = bf16[8,2,4608]{2,1,0:T(2,128)(2,1)S(1)} all-to-all(bf16[8,2,4608]{2,1,0:T(2,128)(2,1)S(1)} %mix_rows.1), channel_id=1, replica_groups=mesh['dp_0'=4,'dp_1'=4,'dp_2'=2,'tensor'=8] {'tensor'}, dimensions={0} | all-to-all | bytes 294912 | tf_op jit(solution)/shard_map/all_to_all | solution.py:159
  38.8 0.0 copy-done.4
  38.8 0.0 copy-done.5
  38.8 0.0 copy-done.3
  38.8 1.0 %hidden_blocks.1 = (bf16[16,16,4736]{2,1,0:T(8,128)(2,1)S(1)}, bf16[16,576]{1,0:T(8,128)(2,1)}) custom-call(bf16[8,2,4608]{2,1,0:T(2,128)(2,1)S(1)} %all_to_all.28.mix_ref, f32[4608]{0:T(1024)S(1)} %copy-done.3, s32[1,16]{1,0:T(1,128)S(1)} %bitcast.14, s32[1,16]{1,0:T(1,128)S(1)} %bitcast.12, s32[1,16]{1,0:T(1,128)S(1)} %bitcast.15), custom_call_target="tpu_custom_call" | custom-call | tf_op jit(solution)/shard_map/hidden_blocks/pallas_call | solution.py:250
  39.8 0.0 copy-start
  39.8 35.1 %all_to_all.29 = bf16[16,16,4736]{2,1,0:T(8,128)(2,1)S(1)} all-to-all(bf16[16,16,4736]{2,1,0:T(8,128)(2,1)S(1)} %get-tuple-element.19), channel_id=1, replica_groups=mesh['dp_0'=4,'dp_1'=4,'dp_2'=2,'tensor'=8] {'dp_0','dp_1'}, dimensions={0} | all-to-all | bytes 4849664 | tf_op jit(solution)/shard_map/all_to_all | solution.py:159
  74.9 0.0 collective-permute-done.1.other_ref
  74.9 0.0 copy-done
  74.9 3.0 %vocab_stats.1 = (f32[128,32]{1,0:T(8,128)S(1)}, s32[1,16]{1,0:T(1,128)}, s32[1,1]{1,0:T(1,128)}) custom-call(bf16[256,4736]{1,0:T(8,128)(2,1)S(1)} %bitcast.10, bf16[512,4608]{1,0:T(8,128)(2,1)S(1)} %copy-done, bf16[512,4608]{1,0:T(8,128)(2,1)S(1)} %collective-permute-done.1.other_ref, s32[1,16]{1,0:T(1,128)S(1)} %bitcast.13), custom_call_target="tpu_custom_call" | custom-call | flops 2415919104 | bytes 9437184 | tf_op jit(solution)/shard_map/vocab_stats/pallas_call | solution.py:319
  77.8 17.5 %all_to_all.30 = f32[128,1,32]{2,1,0:T(1,128)S(1)} all-to-all(f32[128,1,32]{2,1,0:T(1,128)S(1)} %bitcast.11), channel_id=1, replica_groups=mesh['dp_0'=4,'dp_1'=4,'dp_2'=2,'tensor'=8] {'dp_0','dp_1','tensor'}, dimensions={0} | all-to-all | bytes 32768 | tf_op jit(solution)/shard_map/all_to_all | solution.py:159
  95.3 0.1 exponential_reduce_fusion
  95.4 0.5 add_subtract_fusion
  (1 shorter events, 0.0 us)
Async XLA Ops:
  0.6 38.1 %copy-start.4 = (s32[16]{0:T(128)S(1)}, s32[16]{0:T(128)}, u32[]{:S(2)}) copy-start(s32[16]{0:T(128)} %param.25) | copy-start | bytes 196
  0.6 38.1 %copy-start.5 = (s32[16]{0:T(128)S(1)}, s32[16]{0:T(128)}, u32[]{:S(2)}) copy-start(s32[16]{0:T(128)} %param.24) | copy-start | bytes 196
  0.7 26.2 %copy-start.2 = (f32[4608]{0:T(1024)S(1)}, f32[4608]{0:T(1024)}, u32[]{:S(2)}) copy-start(f32[4608]{0:T(1024)} %gain_ref.2) | copy-start | bytes 55300
  0.7 26.2 %copy-start.1 = (bf16[16,4608]{1,0:T(8,128)(2,1)S(1)}, bf16[16,4608]{1,0:T(8,128)(2,1)}, u32[]{:S(2)}) copy-start(bf16[16,4608]{1,0:T(8,128)(2,1)} %residual_ref.1) | copy-start | bytes 442372
  0.7 38.1 %copy-start.3 = (f32[4608]{0:T(1024)S(1)}, f32[4608]{0:T(1024)}, u32[]{:S(2)}) copy-start(f32[4608]{0:T(1024)} %gain_ref.3) | copy-start | bytes 55300
  0.7 7.6 %collective-permute-start = (s32[16]{0:T(128)}, s32[16]{0:T(128)S(1)}, u32[]{:S(2)}, u32[]{:S(2)}) collective-permute-start(s32[16]{0:T(128)} %param.25), channel_id=1, source_target_pairs={{0,8},{8,0},{1,9},{9,1},{2,10},{10,2},{3,11},{11,3},{4,12},{12,4},... | collective-permute-start | bytes 200 | tf_op jit(solution)/shard_map/ppermute | solution.py:163
  8.2 66.6 %collective-permute-start.1 = (bf16[512,4608]{1,0:T(8,128)(2,1)}, bf16[512,4608]{1,0:T(8,128)(2,1)S(1)}, u32[]{:S(2)}, u32[]{:S(2)}) collective-permute-start(bf16[512,4608]{1,0:T(8,128)(2,1)} %own_ref), channel_id=1, source_target_pairs={{0,8},{8,0},{1,9},{9,1},{2,10},{10,2},{3,11},{11,3},{4,12},{12,4},... | collective-permute-start | bytes 14155784 | tf_op jit(solution)/shard_map/ppermute | solution.py:163
  39.8 35.1 %copy-start = (bf16[512,4608]{1,0:T(8,128)(2,1)S(1)}, bf16[512,4608]{1,0:T(8,128)(2,1)}, u32[]{:S(2)}) copy-start(bf16[512,4608]{1,0:T(8,128)(2,1)} %own_ref) | copy-start | bytes 14155780
